TPU v7x, 16 devices: a whole 2x2x2 slice. The times are simulated.
16 devices in a mesh: data: 16 (over z, y, x, core).
Axes of the slice: x: 2, y: 2, z: 2, core: 2. Of those that a mesh axis runs over, the one named last changes fastest.
Arguments:
- z_one: bfloat16 [512, 128], P('data')
- z_two: bfloat16 [512, 128], P('data')
- z_small: bfloat16 [6, 512, 128], P(None, 'data')
- protos: bfloat16 [30000, 128], replicated
- live_mask: int32 [512], P('data')
Outputs:
- output 1: float32 [512, 30000], P('data')
- output 2: float32 [512, 30000], P('data')
- output 3: float32 [], replicated
- output 4: float32 [512, 128], P('data')
- output 5: float32 [512, 128], P('data')
- output 6: float32 [6, 512, 128], P(None, 'data')
- output 7: float32 [30000, 128], replicated
All inputs are finite; a program needn't handle non-finite values.
Results may differ from a plain program's by a relative error of at most 0.001.
Values are sent between devices in bfloat16 or wider.
A program may use at most 1 GiB of HBM per device.

v0:
```python
import jax
import jax.numpy as jnp
from jax import lax
from jax.sharding import PartitionSpec as P

EPS = 0.05
TAU = 0.1
ITERS = 3


def value_a14(scores, live_col, live_total, num_protos):
    weights = live_col * jnp.exp(scores / EPS)
    for step_idx in range(ITERS):
        col_sum = lax.psum(jnp.sum(weights, axis=0), "data")
        weights = weights / (num_protos * col_sum)
        row_sum = jnp.sum(weights, axis=1, keepdims=True)
        row_safe = jnp.where(live_col > 0, row_sum, 1.0)
        weights = weights * (live_col / (live_total * row_safe))
    return live_total * weights


def loss_and_grads(z_one, z_two, z_small, protos, scores_one, scores_two, q_one, q_two, live_col, live_total):
    pair_count = 2 + 2 * z_small.shape[0]
    grad_scale = 1.0 / (TAU * live_total * pair_count)
    scores_small = jnp.einsum("jnd,kd->jnk", z_small, protos, preferred_element_type=jnp.float32)
    logp_one = jax.nn.log_softmax(scores_one / TAU, axis=-1)
    logp_two = jax.nn.log_softmax(scores_two / TAU, axis=-1)
    logp_small = jax.nn.log_softmax(scores_small / TAU, axis=-1)
    q_sum = q_one + q_two
    cross_sum = jnp.sum(q_two * logp_one) + jnp.sum(q_one * logp_two) + jnp.sum(q_sum[None] * logp_small)
    loss_total = -lax.psum(cross_sum, "data") / (live_total * pair_count)
    grad_one = ((live_col * jnp.exp(logp_one) - q_two) * grad_scale).astype(jnp.bfloat16)
    grad_two = ((live_col * jnp.exp(logp_two) - q_one) * grad_scale).astype(jnp.bfloat16)
    grad_small = ((2.0 * live_col[None] * jnp.exp(logp_small) - q_sum[None]) * grad_scale).astype(jnp.bfloat16)
    dz_one = jnp.einsum("nk,kd->nd", grad_one, protos, preferred_element_type=jnp.float32)
    dz_two = jnp.einsum("nk,kd->nd", grad_two, protos, preferred_element_type=jnp.float32)
    dz_small = jnp.einsum("jnk,kd->jnd", grad_small, protos, preferred_element_type=jnp.float32)
    dc_part = (jnp.einsum("nk,nd->kd", grad_one, z_one, preferred_element_type=jnp.float32)
               + jnp.einsum("nk,nd->kd", grad_two, z_two, preferred_element_type=jnp.float32)
               + jnp.einsum("jnk,jnd->kd", grad_small, z_small, preferred_element_type=jnp.float32))
    d_protos = lax.psum(dc_part, "data")
    return loss_total, dz_one, dz_two, dz_small, d_protos


def local_step(z_one, z_two, z_small, protos, live_mask):
    live_f = live_mask.astype(jnp.float32)
    live_col = live_f[:, None]
    live_total = lax.psum(jnp.sum(live_f), "data")
    num_protos = protos.shape[0]
    scores_one = jnp.einsum("nd,kd->nk", z_one, protos, preferred_element_type=jnp.float32)
    q_one = value_a14(scores_one, live_col, live_total, num_protos)
    scores_two = jnp.einsum("nd,kd->nk", z_two, protos, preferred_element_type=jnp.float32)
    q_two = value_a14(scores_two, live_col, live_total, num_protos)
    loss_total, dz_one, dz_two, dz_small, d_protos = loss_and_grads(z_one, z_two, z_small, protos, scores_one, scores_two, q_one, q_two, live_col, live_total)
    return q_one, q_two, loss_total, dz_one, dz_two, dz_small, d_protos


def solution(mesh):
    row_spec = P("data", None)
    crop_spec = P(None, "data", None)
    return jax.shard_map(local_step, mesh=mesh,
                         in_specs=(row_spec, row_spec, crop_spec, P(None, None), P("data")),
                         out_specs=(row_spec, row_spec, P(), row_spec, row_spec, crop_spec, P(None, None)),
                         check_vma=False)
```

profile of v0, /device:TPU:0, one launch (start us, length us, event | category | flops | bytes accessed | tf_op | source)
XLA Modules:
  0.0 688.5 jit_solution(18322080331235369482)
XLA Ops:
  7.9 6.0 multiply_reduce_fusion.4
  13.9 1.9 copy-done.2
  15.8 2.3 exponential_reduce_fusion.2
  18.8 34.7 %psum.63 = f32[]{:T(128)} all-reduce(f32[]{:T(128)} %get-tuple-element.29), channel_id=1, replica_groups=mesh['data'=16] {'data'}, use_global_device_ids=true, to_apply=%region_1.0 | all-reduce | flops 1 | bytes 8 | tf_op jit(solution)/shard_map/psum | solution.py:48
  53.6 32.6 %all-reduce.8.cloned.1.call-done = f32[30000]{0:T(1024)} async-done(((f32[30000]{0:T(1024)}), f32[30000]{0:T(1024)}) %all-reduce.8.cloned.1.call-update) | async-done | bytes 120016 | tf_op jit(solution)/shard_map/psum | solution.py:14
  86.2 0.9 broadcast_multiply_fusion.5
  87.1 3.0 fusion.14
  90.8 1.2 copy-done.11
  92.0 1.1 multiply_reduce_fusion.8
  93.2 7.9 %multiply_reduce_fusion.3 = (f32[32]{0:T(128)S(1)}, f32[32,30000]{1,0:T(8,128)}) fusion(bf16[32,128]{1,0:T(8,128)(2,1)S(1)} %copy-done.15, bf16[30000,128]{1,0:T(8,128)(2,1)} %param.9), kind=kOutput, calls=%fused_computation.20 | convolution fusion | flops 247679968 | bytes 11528320 | tf_op jit(solution)/shard_map/nd,kd->nk/dot_general | solution.py:52
  101.1 55.7 %all-reduce.10.cloned.1.call-done = f32[30000]{0:T(1024)} async-done(((f32[30000]{0:T(1024)}), f32[30000]{0:T(1024)}) %all-reduce.10.cloned.1.call-update) | async-done | bytes 120016 | tf_op jit(solution)/shard_map/psum | solution.py:14
  156.8 0.9 broadcast_multiply_fusion.4
  157.7 2.7 fusion.13
  161.1 1.2 copy-done.5
  162.3 1.1 multiply_reduce_fusion.7
  163.7 2.9 exponential_reduce_fusion.1
  167.3 59.9 %all-reduce.12.cloned.1.call-done = f32[30000]{0:T(1024)} async-done(((f32[30000]{0:T(1024)}), f32[30000]{0:T(1024)}) %all-reduce.12.cloned.1.call-update) | async-done | bytes 120016 | tf_op jit(solution)/shard_map/psum | solution.py:14
  227.2 1.1 broadcast_multiply_fusion.3
  228.3 2.9 fusion.8
  231.8 5.0 multiply_convert_fusion.1
  236.8 2.8 multiply_reduce_fusion.1
  239.6 63.6 %all-reduce.14.cloned.1.call-done = f32[30000]{0:T(1024)} async-done(((f32[30000]{0:T(1024)}), f32[30000]{0:T(1024)}) %all-reduce.14.cloned.1.call-update) | async-done | bytes 120016 | tf_op jit(solution)/shard_map/psum | solution.py:14
  303.3 0.9 broadcast_multiply_fusion.2
  304.2 3.0 fusion.11
  307.9 1.2 copy-done.10
  309.1 1.2 multiply_reduce_fusion.6
  310.4 14.0 %fusion.17 = (f32[6,32]{1,0:T(8,128)S(1)}, f32[6,32,30000]{2,1,0:T(8,128)}) fusion(bf16[6,32,128]{2,1,0:T(8,128)(2,1)S(1)} %copy-done, bf16[30000,128]{1,0:T(8,128)(2,1)} %param.9), kind=kOutput, calls=%fused_computation.58 | convolution fusion | flops 1486079744 | bytes 30769920 | tf_op jit(solution)/shard_map/jnd,kd->jnk/dot_general | solution.py:25
  324.4 49.6 %all-reduce.16.cloned.1.call-done = f32[30000]{0:T(1024)} async-done(((f32[30000]{0:T(1024)}), f32[30000]{0:T(1024)}) %all-reduce.16.cloned.1.call-update) | async-done | bytes 120016 | tf_op jit(solution)/shard_map/psum | solution.py:14
  374.0 0.9 broadcast_multiply_fusion.1
  374.9 2.7 fusion.10
  378.3 1.2 copy-done.6
  379.5 1.2 multiply_reduce_fusion.5
  381.0 10.2 %exponential_reduce_fusion = f32[6,32]{1,0:T(8,128)S(1)} fusion(f32[6,32,30000]{2,1,0:T(8,128)} %get-tuple-element.35, f32[6,32]{1,0:T(8,128)S(1)} %get-tuple-element.34), kind=kLoop, calls=%fused_computation.6 | loop fusion | flops 11519808 | bytes 23041536 | tf_op jit(solution)/shard_map/jit(log_softmax)/reduce_sum | solution.py:28
  391.2 53.2 %all-reduce.18.cloned.1.call-done = f32[30000]{0:T(1024)} async-done(((f32[30000]{0:T(1024)}), f32[30000]{0:T(1024)}) %all-reduce.18.cloned.1.call-update) | async-done | bytes 120016 | tf_op jit(solution)/shard_map/psum | solution.py:14
  444.4 1.1 broadcast_multiply_fusion
  445.4 2.8 fusion.9
  448.9 4.3 multiply_convert_fusion.2
  453.3 2.4 fusion.16
  455.7 12.4 %multiply_convert_fusion = (bf16[6,32,30000]{2,1,0:T(8,128)(2,1)S(1)}, f32[]{:T(128)}) fusion(f32[6,32,30000]{2,1,0:T(8,128)} %get-tuple-element.35, f32[]{:T(128)S(6)} %div.121, f32[32]{0:T(128)S(1)} %get-tuple-element.28, f32[6,32]{1,0:T(8,128)S(1)} %log.17, f32[6,32]{1,0:T(8,128)S(1)} %get-tuple-element.34, f32[32,30000]{1,0:T(8,128)S(1)} %get-tuple-element.26), kind=kLoop, calls=%fused_computation.4 | loop fusion | flops 46080000 | bytes 38401672 | tf_op jit(solution)/shard_map/convert_element_type | solution.py:34
  468.0 8.4 %convolution_bitcast_fusion = f32[30000,128]{1,0:T(8,128)} fusion(bf16[6,32,30000]{2,1,0:T(8,128)(2,1)S(1)} %get-tuple-element.24, bf16[6,32,128]{2,1,0:T(8,128)(2,1)S(1)} %copy-done), kind=kOutput, calls=%fused_computation.3 | convolution fusion | flops 1474560000 | bytes 26929152 | tf_op jit(solution)/shard_map/jnk,jnd->kd/dot_general | solution.py:40
  477.0 6.6 fusion.20
  483.7 16.9 %fusion = f32[30000,128]{1,0:T(8,128)} fusion(f32[30000,128]{1,0:T(8,128)} %convolution_bitcast_fusion, f32[30000,128]{1,0:T(8,128)} %fusion.20, bf16[32,30000]{1,0:T(8,128)(2,1)S(1)} %copy-done.12, bf16[32,128]{1,0:T(8,128)(2,1)S(1)} %copy-done.15), kind=kOutput, calls=%fused_computation.2 | convolution fusion | flops 253440000 | bytes 48008192 | tf_op jit(solution)/shard_map/nk,nd->kd/dot_general | solution.py:39
  503.2 5.7 fusion.19
  508.9 31.9 %psum.70 = f32[]{:T(128)} all-reduce(f32[]{:T(128)S(6)} %add.35), channel_id=1, replica_groups=mesh['data'=16] {'data'}, use_global_device_ids=true, to_apply=%region_27.29 | all-reduce | flops 1 | bytes 8 | tf_op jit(solution)/shard_map/psum | solution.py:31
  541.5 5.1 fusion.18
  546.6 10.3 %fusion.1 = f32[6,32,128]{2,1,0:T(8,128)} fusion(bf16[6,32,30000]{2,1,0:T(8,128)(2,1)} %copy-done.7, bf16[30000,128]{1,0:T(8,128)(2,1)} %param.9), kind=kOutput, calls=%fused_computation.7 | convolution fusion | flops 1474560000 | bytes 19298304 | tf_op jit(solution)/shard_map/jnk,kd->jnd/dot_general | solution.py:37
  556.9 112.8 %all-reduce.20.cloned.1.call-done = f32[30000,128]{1,0:T(8,128)} async-done(((f32[30000,128]{1,0:T(8,128)}), f32[30000,128]{1,0:T(8,128)}) %all-reduce.20.cloned.1.call-update) | async-done | bytes 15360016 | tf_op jit(solution)/shard_map/psum | solution.py:41
  669.7 10.8 %copy.19 = f32[30000,128]{1,0:T(8,128)} copy(f32[30000,128]{1,0:T(8,128)} %all-reduce.20.cloned.1.call-done) | data formatting | bytes 30720000
  (54 shorter events, 6.8 us)
Async XLA Ops:
  7.2 303.2 %copy-start = (bf16[6,32,128]{2,1,0:T(8,128)(2,1)S(1)}, bf16[6,32,128]{2,1,0:T(8,128)(2,1)}, u32[]{:S(2)}) copy-start(bf16[6,32,128]{2,1,0:T(8,128)(2,1)} %param.8) | copy-start | bytes 147460
  7.2 79.0 %all-reduce.8.cloned.1.call-start = ((), (), s32[]{:S(2)}) async-start(), calls=%async_computation | async-start | bytes 245760 | tf_op jit(solution)/shard_map/psum | solution.py:14
  13.9 1.9 copy-start.2
  13.9 4.3 copy-start.16
  18.2 138.7 %all-reduce.10.cloned.1.call-start = ((), (), s32[]{:S(2)}) async-start(), calls=%async_computation.1 | async-start | bytes 245760 | tf_op jit(solution)/shard_map/psum | solution.py:14
  90.1 1.9 copy-start.11
  90.1 3.1 copy-start.15
  93.2 134.0 %all-reduce.12.cloned.1.call-start = ((), (), s32[]{:S(2)}) async-start(), calls=%async_computation.2 | async-start | bytes 245760 | tf_op jit(solution)/shard_map/psum | solution.py:14
  160.4 1.9 copy-start.5
  163.5 139.8 %all-reduce.14.cloned.1.call-start = ((), (), s32[]{:S(2)}) async-start(), calls=%async_computation.3 | async-start | bytes 245760 | tf_op jit(solution)/shard_map/psum | solution.py:14
  227.2 4.6 copy-start.4
  236.8 2.8 copy-start.8
  239.6 134.4 %all-reduce.16.cloned.1.call-start = ((), (), s32[]{:S(2)}) async-start(), calls=%async_computation.4 | async-start | bytes 245760 | tf_op jit(solution)/shard_map/psum | solution.py:14
  307.2 1.9 copy-start.10
  310.3 134.1 %all-reduce.18.cloned.1.call-start = ((), (), s32[]{:S(2)}) async-start(), calls=%async_computation.5 | async-start | bytes 245760 | tf_op jit(solution)/shard_map/psum | solution.py:14
  377.6 1.9 copy-start.6
  380.7 289.0 %all-reduce.20.cloned.1.call-start = ((), (), s32[]{:S(2)}) async-start(), calls=%async_computation.6 | async-start | bytes 30720000 | tf_op jit(solution)/shard_map/psum | solution.py:41
  444.4 4.5 copy-start.3
  448.9 4.3 copy-start.9
  453.2 2.4 copy-start.13
  468.0 9.0 %copy-start.7 = (bf16[6,32,30000]{2,1,0:T(8,128)(2,1)}, bf16[6,32,30000]{2,1,0:T(8,128)(2,1)S(1)}, u32[]{:S(2)}) copy-start(bf16[6,32,30000]{2,1,0:T(8,128)(2,1)S(1)} %get-tuple-element.24) | copy-start | bytes 34560004
  468.0 9.0 %copy-start.14 = (bf16[32,128]{1,0:T(8,128)(2,1)S(1)}, bf16[32,128]{1,0:T(8,128)(2,1)}, u32[]{:S(2)}) copy-start(bf16[32,128]{1,0:T(8,128)(2,1)} %param.6) | copy-start | bytes 24580
  477.0 6.6 copy-start.12
  669.7 10.8 %copy-start.1 = (bf16[6,32,128]{2,1,0:T(8,128)(2,1)S(1)}, bf16[6,32,128]{2,1,0:T(8,128)(2,1)}, u32[]{:S(2)}) copy-start(bf16[6,32,128]{2,1,0:T(8,128)(2,1)} %param.8) | copy-start | bytes 147460
Sparse Core Ops, SparseCore 0:
  18.3 67.8 all-reduce.7
  93.3 63.4 all-reduce.9
  163.6 63.5 all-reduce.11
  239.7 63.5 all-reduce.13
  310.4 63.5 all-reduce.15
  380.8 63.5 all-reduce.17
  500.8 168.9 all-reduce.19
where the time goes:
time: 690 us; the launch traced here: 688 us
  waiting for transfers between devices  428 us (62%)
  matrix products  81 us (12%)
  other arithmetic  75 us (11%)
  blocking collectives  66.6 us (10%)
  between operations  19.5 us (3%)
  local copies, waits for them, and re-layouts  18.3 us (3%)
    psum x6, waiting for transfers between devices, value_a14(): col_sum = lax.psum(jnp.sum(weights, axis=0), 'data')  315 us
    psum x1, waiting for transfers between devices, loss_and_grads(): d_protos = lax.psum(dc_part, 'data')  113 us
    psum x1, blocking collectives, local_step(): live_total = lax.psum(jnp.sum(live_f), 'data')  34.7 us
    psum x1, blocking collectives, loss_and_grads(): loss_total = -lax.psum(cross_sum, 'data') / (live_total * pair_count)  31.9 us
    unnamed x35, local copies, waits for them, and re-layouts  18.3 us
    reduce_sum x6, other arithmetic, value_a14(): row_sum = jnp.sum(weights, axis=1, keepdims=True)  17.1 us
    dot_general x1, matrix products, loss_and_grads(): jnp.einsum('nk,nd->kd', grad_two, z_two, preferred_element_type=jnp.float32)  16.9 us
    dot_general x1, matrix products, loss_and_grads(): jnp.einsum('jnd,kd->jnk', z_small, protos, preferred_element_type=jnp.flo...  14 us
  transfers between devices with their start and end apart: 7, of which 7 were waited for; matrix products, arithmetic and copies ran while one was open for 8% of the time, Pallas kernels for 0%

commit v1 on v0

v1 whole, which is shorter than its diff:
```python
import functools

import jax
import jax.numpy as jnp
import numpy as np
from jax import lax
from jax.experimental import pallas as pl
from jax.experimental.pallas import tpu as pltpu
from jax.sharding import PartitionSpec as P

TAU = 0.1
LOG2E = 1.4426950408889634
LN2 = 0.6931471805599453
SCALE = LOG2E / TAU
NDEV = 16
ROWS = 32
NS = 512
VIEWS = 8
D = 128
KP = 30000
SH = 1920
KPAD = SH * NDEV
LAST = KP - SH * (NDEV - 1)
CB = 384
NCH = SH // CB
PAIRS = 14.0
LOGICAL = pl.DeviceIdType.LOGICAL
VM = 60 * 1024 * 1024


def dot_nt(a, b):
    return lax.dot_general(a, b, (((1,), (1,)), ((), ())), preferred_element_type=jnp.float32)


def dot_nn(a, b):
    return lax.dot_general(a, b, (((1,), (0,)), ((), ())), preferred_element_type=jnp.float32)


def fold8(x):
    return jnp.sum(x.reshape(x.shape[0] // 8, 8, x.shape[1]), axis=0)


def flip(me, bit):
    return me + bit - 2 * bit * lax.rem(me // bit, 2)


def full_barrier(me):
    barrier = pltpu.get_barrier_semaphore()
    for d in range(1, NDEV):
        pl.semaphore_signal(barrier, inc=1, device_id=lax.rem(me + d, NDEV), device_id_type=LOGICAL)
    pl.semaphore_wait(barrier, NDEV - 1)


def send(src, dst, ssem, rsem, to):
    copy = pltpu.make_async_remote_copy(src_ref=src, dst_ref=dst, send_sem=ssem, recv_sem=rsem,
                                        device_id=to, device_id_type=LOGICAL)
    copy.start()


def drain(ref, sem):
    pltpu.make_async_copy(ref, ref, sem).wait()


def load_shard(me, protos, cs, sem, start):
    @pl.when(me < NDEV - 1)
    def _():
        c = pltpu.make_async_copy(protos.at[pl.ds(pl.multiple_of(me * SH, 8), SH)], cs, sem)
        c.start() if start else c.wait()

    @pl.when(me == NDEV - 1)
    def _():
        c = pltpu.make_async_copy(protos.at[pl.ds(SH * (NDEV - 1), LAST)], cs.at[pl.ds(0, LAST)], sem)
        if start:
            c.start()
            cs[pl.ds(LAST, SH - LAST), :] = jnp.zeros((SH - LAST, D), jnp.bfloat16)
        else:
            c.wait()


def sk_kernel(z1, z2, zs, m8, protos, zall, arow, brow, wall, lout,
              cs, ex, slots, lslots, csem, zsend, zlrecv, zs1recv, zs2send, zs2recv,
              arsend, arrecv, lsend, lrecv, wsend, wrecv):
    me = lax.axis_index("data")
    load_shard(me, protos, cs, csem, True)
    full_barrier(me)
    myrows = pl.ds(pl.multiple_of(me * ROWS, ROWS), ROWS)
    slots[0, me] = m8[...]
    for d in range(1, NDEV):
        to = lax.rem(me + d, NDEV)
        send(m8, slots.at[0, me], arsend.at[0], arrecv.at[0], to)
        send(z1, zall.at[0, myrows], zsend.at[0], zlrecv, to)
        send(z2, zall.at[1, myrows], zsend.at[0], zlrecv, to)
    for d in range(1, NDEV // 2):
        to = lax.rem(me + 2 * d, NDEV)
        send(zs, zall.at[pl.ds(2, 6), myrows], zsend.at[1], zs1recv, to)
    sib = flip(me, 1)
    zall[0, myrows] = z1[...]
    zall[1, myrows] = z2[...]
    zall[pl.ds(2, 6), myrows] = zs[...]
    send(zs, zall.at[pl.ds(2, 6), myrows], zs2send, zs2recv, sib)
    load_shard(me, protos, cs, csem, False)

    def ar_send(t):
        for d in range(1, NDEV):
            send(slots.at[t, me], slots.at[t, me], arsend.at[t], arrecv.at[t], lax.rem(me + d, NDEV))

    def ar_total(t):
        drain(slots.at[t, pl.ds(0, NDEV - 1)], arrecv.at[t])
        tot = slots[t, 0]
        for i in range(1, NDEV):
            tot = tot + slots[t, i]
        return tot

    mask8 = ar_total(0)
    live = jnp.sum(jnp.sum(mask8, axis=1, keepdims=True), axis=0, keepdims=True)
    mrow = jnp.concatenate([mask8[j:j + 1] for j in range(4)], axis=1)
    drain(zall.at[pl.ds(0, 2), pl.ds(0, NS - ROWS)], zlrecv)

    def col_scale(c, b):
        k = me * SH + b * CB + lax.broadcasted_iota(jnp.int32, (CB, 1), 0)
        return jnp.where(k < KP, 1.0 / (KP * c), 0.0)

    zero8 = jnp.zeros((8, NS), jnp.float32)

    def first(b, carry):
        rows = pl.ds(pl.multiple_of(b * CB, CB), CB)
        out = []
        for v in range(2):
            ps, r = carry[2 * v], carry[2 * v + 1]
            p = jnp.exp2(dot_nt(cs[rows], zall[v]) * SCALE)
            ps = ps + fold8(p)
            e = p * p * mrow
            ex[v, rows] = e
            w = col_scale(jnp.sum(e, axis=1, keepdims=True), b)
            r = r + fold8(e * w)
            out += [ps, r]
        return tuple(out)

    def put(t, r1, r2):
        for v, r in enumerate((r1, r2)):
            row = jnp.sum(r, axis=0, keepdims=True)
            for j in range(4):
                slots[t, me, pl.ds(4 * v + j, 1)] = row[:, 128 * j:128 * (j + 1)]

    def scale_rows(tot):
        us = []
        for v in range(2):
            r = jnp.concatenate([tot[4 * v + j:4 * v + j + 1] for j in range(4)], axis=1)
            us.append(mrow / (live * jnp.where(mrow > 0, r, 1.0)))
        return us

    pad = jnp.where(me == NDEV - 1, float(SH - LAST), 0.0)

    def put_lse(v, ps):
        row = jnp.sum(ps, axis=0, keepdims=True) - pad
        for j in range(4):
            lslots[me, pl.ds(4 * v + j, 1)] = row[:, 128 * j:128 * (j + 1)]

    ps1, r1, ps2, r2 = lax.fori_loop(0, NCH, first, (zero8, zero8, zero8, zero8))
    put(1, r1, r2)
    ar_send(1)
    put_lse(0, ps1)
    put_lse(1, ps2)
    drain(zall.at[pl.ds(2, 6), pl.ds(0, 7 * ROWS)], zs1recv)
    for d in range(1, NDEV // 2):
        rows = pl.ds(pl.multiple_of(lax.rem(me + 2 * d, NDEV) * ROWS, ROWS), ROWS)
        send(zall.at[pl.ds(2, 6), rows], zall.at[pl.ds(2, 6), rows], zs2send, zs2recv, sib)
    us = scale_rows(ar_total(1))

    def again(us, last):
        def step(b, carry):
            rows = pl.ds(pl.multiple_of(b * CB, CB), CB)
            out = []
            for v in range(2):
                e = ex[v, rows]
                w = col_scale(jnp.sum(e * us[v], axis=1, keepdims=True), b)
                out.append(carry[v] + fold8(e * w))
                if last:
                    for q in range(CB // 128):
                        wt = jnp.broadcast_to(w[128 * q:128 * (q + 1)], (128, 128)).T
                        wall[me, pl.ds(v, 1), pl.ds(pl.multiple_of(b * CB + 128 * q, 128), 128)] = wt[0:1]
            return tuple(out)
        return step

    r1, r2 = lax.fori_loop(0, NCH, again(us, False), (zero8, zero8))
    put(2, r1, r2)
    ar_send(2)
    drain(zall.at[pl.ds(2, 6), pl.ds(0, 8 * ROWS)], zs2recv)

    def small(i, carry):
        v = 2 + i

        def blk(b, ps):
            rows = pl.ds(pl.multiple_of(b * CB, CB), CB)
            return ps + fold8(jnp.exp2(dot_nt(cs[rows], zall[v]) * SCALE))

        ps = lax.fori_loop(0, NCH, blk, zero8)
        row = jnp.sum(ps, axis=0, keepdims=True) - pad
        for j in range(4):
            lslots[me, pl.ds(4 * v + j, 1)] = row[:, 128 * j:128 * (j + 1)]
        return carry

    lax.fori_loop(0, 6, small, 0)
    us = scale_rows(ar_total(2))
    r1, r2 = lax.fori_loop(0, NCH, again(us, True), (zero8, zero8))
    put(3, r1, r2)
    ar_send(3)
    for d in range(1, NDEV):
        to = lax.rem(me + d, NDEV)
        send(lslots.at[me], lslots.at[me], lsend, lrecv, to)
    for d in range(1, NDEV):
        to = lax.rem(me + d, NDEV)
        send(wall.at[me], wall.at[me], wsend, wrecv, to)
    us = scale_rows(ar_total(3))
    gs = 1.0 / (TAU * PAIRS * live)
    for v in range(2):
        brow[v:v + 1] = gs * live * us[v]
        brow[v + 2:v + 3] = live * us[v]
    brow[4:8] = jnp.zeros((4, NS), jnp.float32)
    drain(lslots.at[pl.ds(0, NDEV - 1)], lrecv)
    tot = lslots[0]
    for i in range(1, NDEV):
        tot = tot + lslots[i]
    inv = 1.0 / tot
    for v in range(VIEWS):
        for j in range(4):
            coef = 1.0 if v < 2 else 2.0
            arow[v:v + 1, 128 * j:128 * (j + 1)] = (coef * gs) * (mask8[j:j + 1] * inv[4 * v + j:4 * v + j + 1])
    weight = jnp.concatenate([mask8[0:4]] * 2 + [2.0 * mask8[0:4]] * 6, axis=0)
    lsum = jnp.sum(jnp.sum(weight * jnp.log(tot), axis=1, keepdims=True), axis=0, keepdims=True)
    lout[0:1] = jnp.broadcast_to(lsum, (1, 128))
    lout[1:2] = jnp.broadcast_to(live, (1, 128))
    lout[2:8] = jnp.zeros((6, 128), jnp.float32)
    drain(wall.at[pl.ds(0, NDEV - 1)], wrecv)
    drain(zall.at[pl.ds(0, 2), pl.ds(0, NS - ROWS)], zsend.at[0])
    drain(zall.at[pl.ds(2, 6), pl.ds(0, 7 * ROWS)], zsend.at[1])
    drain(zall.at[pl.ds(2, 6), pl.ds(0, 8 * ROWS)], zs2send)
    for t in range(4):
        drain(slots.at[t, pl.ds(0, NDEV - 1)], arsend.at[t])
    drain(lslots.at[pl.ds(0, NDEV - 1)], lsend)
    drain(wall.at[pl.ds(0, NDEV - 1)], wsend)


RB = 512
NIT = 15
RPI = KPAD // RB // NIT


def grad_kernel(zall, arow, brow, wall, lout, z1, z2, zs, protos, dc, dz1, dz2, dzs, loss,
                ca, gt, zl, cols, acc, lslots, csem, ssem, r1, r2, r3, rs, lsend, lrecv):
    me = lax.axis_index("data")
    cc = pltpu.make_async_copy(protos, ca.at[pl.ds(0, KP)], csem)
    cc.start()
    ca[pl.ds(KP, KPAD - KP), :] = jnp.zeros((KPAD - KP, D), jnp.bfloat16)
    full_barrier(me)
    dims = (flip(me, 2), flip(me, 4), flip(me, 8))
    sib = flip(me, 1)
    zl[pl.ds(0, ROWS)] = z1[...]
    zl[pl.ds(ROWS, ROWS)] = z2[...]
    zl[pl.ds(2 * ROWS, 6 * ROWS)] = zs[...].reshape(6 * ROWS, D)
    tile = pl.ds(pl.multiple_of((me // 4) * 128, 128), 128)
    cols[0] = jnp.broadcast_to(arow[:, tile].T, (128, 8))
    cols[1] = jnp.broadcast_to(brow[:, tile].T, (128, 8))
    acc[...] = jnp.zeros_like(acc)
    mine = pl.ds(pl.multiple_of(lax.rem(me, 4) * ROWS, ROWS), ROWS)
    ac = cols[0, mine]
    bc = cols[1, mine]
    cc.wait()

    def piece(owner, t, a):
        return dc.at[pl.ds(pl.multiple_of(owner * SH + t * CB + a * 128, 128), 128)]

    def push(owner, t, a, to, rsem):
        ref = piece(owner, t, a)
        send(ref, ref, ssem.at[t, a], rsem.at[t, a], to)

    def chunk(owner, t):
        base = pl.multiple_of(owner * SH + t * CB, 128)
        c = ca[pl.ds(base, CB)]
        wc = []
        for v in range(2):
            parts = []
            for q in range(CB // 128):
                off = pl.multiple_of(t * CB + q * 128, 128)
                row = wall[owner, pl.ds(v, 1), pl.ds(off, 128)]
                parts.append(jnp.broadcast_to(row, (128, 128)).T)
            wc.append(jnp.concatenate(parts, axis=0))

        def nblk(nb, carry):
            ln = pl.ds(pl.multiple_of(nb * 256, 256), 256)
            s = [dot_nt(c, zall[v, ln]) for v in range(VIEWS)]
            av = [arow[v:v + 1, ln] for v in range(VIEWS)]
            bv = [brow[v:v + 1, ln] for v in range(2)]
            for q in range(CB // 64):
                sl = slice(64 * q, 64 * (q + 1))
                w0 = jnp.concatenate([wc[0][sl], wc[0][sl]], axis=1)
                w1 = jnp.concatenate([wc[1][sl], wc[1][sl]], axis=1)
                p0 = jnp.exp2(s[0][sl] * SCALE)
                p1 = jnp.exp2(s[1][sl] * SCALE)
                x0 = (p0 * p0) * bv[0] * w0
                x1 = (p1 * p1) * bv[1] * w1
                xs = x0 + x1
                gs = [p0 * av[0] - x1, p1 * av[1] - x0]
                for v in range(2, VIEWS):
                    gs.append(jnp.exp2(s[v][sl] * SCALE) * av[v] - xs)
                for v in range(VIEWS):
                    gt[pl.ds(64 * q, 64), pl.ds(pl.multiple_of(v * NS + nb * 256, 256), 256)] = gs[v].astype(jnp.bfloat16)
            return carry

        lax.fori_loop(0, 2, nblk, 0)
        dc[pl.ds(base, CB)] = dot_nn(gt[...], zall[...].reshape(VIEWS * NS, D))

    def row_block(j, carry):
        base = pl.multiple_of(j * RB, RB)
        c = ca[pl.ds(base, RB)]
        s = dot_nt(zl[...], c) * SCALE
        sh = j // (SH // RB) if SH % RB == 0 else 0
        return carry, s, sh

    def rows_part(i):
        for h in range(RPI):
            base = pl.multiple_of(i * (RPI * RB) + h * RB, RB)
            c = ca[pl.ds(base, RB)]
            s = dot_nt(zl[...], c) * SCALE
            wr = []
            for v in range(2):
                parts = []
                for q in range(RB // 128):
                    b = i * (RPI * RB // 128) + h * (RB // 128) + q
                    parts.append(wall[b // (SH // 128), pl.ds(v, 1), pl.ds(pl.multiple_of(lax.rem(b, SH // 128) * 128, 128), 128)])
                wr.append(jnp.concatenate(parts, axis=1))
            sv = [s[ROWS * v:ROWS * (v + 1)] for v in range(VIEWS)]
            p0 = jnp.exp2(sv[0])
            p1 = jnp.exp2(sv[1])
            x0 = (p0 * p0) * bc[:, 0:1] * wr[0]
            x1 = (p1 * p1) * bc[:, 1:2] * wr[1]
            xs = x0 + x1
            gs = [p0 * ac[:, 0:1] - x1, p1 * ac[:, 1:2] - x0]
            ssum = sv[2]
            for v in range(3, VIEWS):
                ssum = ssum + sv[v]
            for v in range(2, VIEWS):
                gs.append(jnp.exp2(sv[v]) * ac[:, v:v + 1] - xs)
            g = jnp.concatenate([x.astype(jnp.bfloat16) for x in gs], axis=0)
            acc[pl.ds(0, VIEWS * ROWS)] += dot_nn(g, c)
            ls = x1 * sv[0] + x0 * sv[1] + xs * ssum
            part = ls[:, 0:128]
            for q in range(1, RB // 128):
                part = part + ls[:, 128 * q:128 * (q + 1)]
            acc[pl.ds(VIEWS * ROWS, ROWS)] += part

    def order(a):
        return dims[a], dims[(a + 1) % 3], dims[(a + 2) % 3]

    def own(t):
        for a in range(3):
            d0, d1, d2 = order(a)
            push(me, t, a, d0, r1)
            push(me, t, a, d1, r2)
            push(me, t, a, d2, r3)
            push(me, t, a, sib, rs)

    def serve1(t):
        for a in range(3):
            d0, d1, d2 = order(a)
            drain(piece(me, t, a), r1.at[t, a])
            push(d0, t, a, d1, r2)
            push(d0, t, a, d2, r3)
            push(d0, t, a, sib, rs)

    def serve2(t):
        for a in range(3):
            d0, d1, d2 = order(a)
            drain(dc.at[pl.ds(0, 256)], r2.at[t, a])
            d10 = d0 + d1 - me
            for o in (d1, d10):
                push(o, t, a, d2, r3)
                push(o, t, a, sib, rs)

    def serve3(t):
        for a in range(3):
            d0, d1, d2 = order(a)
            drain(dc.at[pl.ds(0, 512)], r3.at[t, a])
            for o in (d2, d2 + d0 - me, d2 + d1 - me, d2 + d1 + d0 - 2 * me):
                push(o, t, a, sib, rs)

    def main(it, carry):
        @pl.when(it < NCH)
        def _():
            chunk(me, it)
            own(it)

        rows_part(it)

        @pl.when(jnp.logical_and(it >= 2, it < 2 + NCH))
        def _():
            serve1(it - 2)

        @pl.when(jnp.logical_and(it >= 6, it < 6 + NCH))
        def _():
            serve2(it - 6)

        @pl.when(jnp.logical_and(it >= 9, it < 9 + NCH))
        def _():
            serve3(it - 9)

        return carry

    lax.fori_loop(0, NIT, main, 0)

    total = jnp.sum(jnp.sum(acc[pl.ds(VIEWS * ROWS, ROWS)], axis=1, keepdims=True), axis=0, keepdims=True)
    lslots[me] = jnp.broadcast_to(total, (8, 128))
    for d in range(1, NDEV):
        send(lslots.at[me], lslots.at[me], lsend, lrecv, lax.rem(me + d, NDEV))
    dz1[...] = acc[pl.ds(0, ROWS)]
    dz2[...] = acc[pl.ds(ROWS, ROWS)]
    dzs[...] = acc[pl.ds(2 * ROWS, 6 * ROWS)].reshape(6, ROWS, D)
    drain(lslots.at[pl.ds(0, NDEV - 1)], lrecv)
    tot = lslots[0]
    for i in range(1, NDEV):
        tot = tot + lslots[i]
    live = lout[1:2]
    cross = tot[0:1] * (LN2 * TAU * PAIRS) * live - lout[0:1]
    loss[...] = jnp.broadcast_to(-cross / (live * PAIRS), (8, 128))
    drain(lslots.at[pl.ds(0, NDEV - 1)], lsend)

    def finish(t, carry):
        for a in range(3):
            drain(dc.at[pl.ds(0, 8 * 128)], rs.at[t, a])
            drain(dc.at[pl.ds(0, 15 * 128)], ssem.at[t, a])
        return carry

    lax.fori_loop(0, NCH, finish, 0)


QB = 2048


def q_kernel(z1, z2, bcol, c, w, q1, q2):
    for v, (z, q) in enumerate(((z1, q1), (z2, q2))):
        p = jnp.exp2(dot_nt(z[...], c[...]) * SCALE)
        q[...] = (p * p) * bcol[:, v:v + 1] * w[v:v + 1]


def local_step(z_one, z_two, z_small, protos, live_mask):
    me = lax.axis_index("data")
    live_f = live_mask.astype(jnp.float32)
    pos = jnp.arange(1024, dtype=jnp.int32).reshape(8, 128) // ROWS
    m8 = jnp.where(pos == me, jnp.tile(live_f, 4)[None, :], 0.0)
    f32 = jnp.float32
    vmem = pl.BlockSpec(memory_space=pltpu.VMEM)
    anym = pl.BlockSpec(memory_space=pl.ANY)
    dma = pltpu.SemaphoreType.DMA
    zall, arow, brow, wall, lout = pl.pallas_call(
        sk_kernel,
        out_shape=[jax.ShapeDtypeStruct((VIEWS, NS, D), jnp.bfloat16), jax.ShapeDtypeStruct((8, NS), f32),
                   jax.ShapeDtypeStruct((8, NS), f32), jax.ShapeDtypeStruct((NDEV, 2, SH), f32),
                   jax.ShapeDtypeStruct((8, 128), f32)],
        in_specs=[vmem, vmem, vmem, vmem, anym],
        out_specs=[vmem] * 5,
        scratch_shapes=[pltpu.VMEM((SH, D), jnp.bfloat16), pltpu.VMEM((2, SH, NS), f32),
                        pltpu.VMEM((4, NDEV, 8, 128), f32), pltpu.VMEM((NDEV, 32, 128), f32),
                        dma, dma((2,)), dma, dma, dma, dma, dma((4,)), dma((4,)), dma, dma, dma, dma],
        compiler_params=pltpu.CompilerParams(collective_id=0, has_side_effects=True, vmem_limit_bytes=VM),
        name="sinkhorn",
    )(z_one, z_two, z_small, m8, protos)

    dcp, dz1, dz2, dzs, loss = pl.pallas_call(
        grad_kernel,
        out_shape=[jax.ShapeDtypeStruct((KPAD, D), f32), jax.ShapeDtypeStruct((ROWS, D), f32),
                   jax.ShapeDtypeStruct((ROWS, D), f32), jax.ShapeDtypeStruct((6, ROWS, D), f32),
                   jax.ShapeDtypeStruct((8, 128), f32)],
        in_specs=[vmem] * 8 + [anym],
        out_specs=[vmem] * 5,
        scratch_shapes=[pltpu.VMEM((KPAD, D), jnp.bfloat16), pltpu.VMEM((CB, VIEWS * NS), jnp.bfloat16),
                        pltpu.VMEM((VIEWS * ROWS, D), jnp.bfloat16), pltpu.VMEM((2, 128, 8), f32),
                        pltpu.VMEM((VIEWS * ROWS + ROWS, D), f32), pltpu.VMEM((NDEV, 8, 128), f32),
                        dma, dma((NCH, 3)), dma((NCH, 3)), dma((NCH, 3)), dma((NCH, 3)), dma((NCH, 3)), dma, dma],
        compiler_params=pltpu.CompilerParams(collective_id=1, has_side_effects=True, vmem_limit_bytes=VM),
        name="grads",
    )(zall, arow, brow, wall, lout, z_one, z_two, z_small, protos)

    bcol = lax.dynamic_slice(brow, (2, me * ROWS), (2, ROWS)).T
    w2 = jnp.swapaxes(wall, 0, 1).reshape(2, KPAD)
    q1, q2 = pl.pallas_call(
        q_kernel,
        grid=(pl.cdiv(KP, QB),),
        out_shape=[jax.ShapeDtypeStruct((ROWS, KP), f32)] * 2,
        in_specs=[pl.BlockSpec((ROWS, D), lambda j: (0, 0)), pl.BlockSpec((ROWS, D), lambda j: (0, 0)),
                  pl.BlockSpec((ROWS, 2), lambda j: (0, 0)), pl.BlockSpec((QB, D), lambda j: (j, 0)),
                  pl.BlockSpec((2, QB), lambda j: (0, j))],
        out_specs=[pl.BlockSpec((ROWS, QB), lambda j: (0, j))] * 2,
        compiler_params=pltpu.CompilerParams(dimension_semantics=("arbitrary",)),
        name="codes",
    )(z_one, z_two, bcol, protos, w2)
    return q1, q2, loss[0, 0], dz1, dz2, dzs, dcp[:KP]


def solution(mesh):
    row_spec = P("data", None)
    crop_spec = P(None, "data", None)
    return jax.shard_map(local_step, mesh=mesh,
                         in_specs=(row_spec, row_spec, crop_spec, P(None, None), P("data")),
                         out_specs=(row_spec, row_spec, P(), row_spec, row_spec, crop_spec, P(None, None)),
                         check_vma=False)
```

time: 690 us -> 142 us (0.21)
  waiting for transfers between devices: 428 us -> 0 us
  Pallas kernels: 0 us -> 125 us
  matrix products: 81 us -> 0 us
  other arithmetic: 75 us -> 1.27 us
  blocking collectives: 66.6 us -> 0 us
  between operations: 19.5 us -> 0.68 us
    psum x7 -> x0, waiting for transfers between devices: 427 us -> none  [the longest x6 315 us: value_a14(): col_sum = lax.psum(jnp.sum(weights, axis=0), 'data')]
    pallas_call x0 -> x3, Pallas kernels: none -> 125 us  [the longest x1 70.7 us: local_step(): pl.pallas_call(grad_kernel, out_shape=[jax.ShapeDtypeStruct((KPAD, D), f3...]
    dot_general x9 -> x0, matrix products: 81 us -> none  [the longest x1 16.9 us: loss_and_grads(): jnp.einsum('nk,nd->kd', grad_two, z_two, preferred_element_type=jnp.float32)]
    psum x2 -> x0, blocking collectives: 66.6 us -> none  [the longest x1 34.7 us: local_step(): live_total = lax.psum(jnp.sum(live_f), 'data')]
    reduce_sum x14 -> x0, other arithmetic: 39.9 us -> none  [the longest x6 17.1 us: value_a14(): row_sum = jnp.sum(weights, axis=1, keepdims=True)]
    convert_element_type x3 -> x0, other arithmetic: 21.6 us -> none  [the longest x1 12.4 us: loss_and_grads(): ((2.0 * live_col[None] * jnp.exp(logp_small) - q_sum[None]) * grad_scale)...]
    unnamed x35 -> x11, local copies, waits for them, and re-layouts: 18.3 us -> 1.87 us
    slice x0 -> x2, local copies, waits for them, and re-layouts: none -> 12 us  [local_step(): return (q1, q2, loss[0, 0], dz1, dz2, dzs, dcp[:KP])]
  transfers between devices with their start and end apart: 7 -> 0, of which waited for: 7 -> 0; matrix products, arithmetic and copies ran while one was open for 8% -> 0% of each run, Pallas kernels for 0% -> 0%
where the time goes in v1:
time: 142 us; the launch traced here: 141 us
  Pallas kernels  125 us (88%)
  local copies, waits for them, and re-layouts  14.8 us (10%)
    pallas_call x1, Pallas kernels, local_step(): pl.pallas_call(grad_kernel, out_shape=[jax.ShapeDtypeStruct((KPAD, D), f3...  70.7 us
    pallas_call x1, Pallas kernels, local_step(): pl.pallas_call(sk_kernel, out_shape=[jax.ShapeDtypeStruct((VIEWS, NS, D),...  39.5 us
    pallas_call x1, Pallas kernels, local_step(): pl.pallas_call(q_kernel, grid=(pl.cdiv(KP, QB),), out_shape=[jax.ShapeDty...  14.4 us
    slice x2, local copies, waits for them, and re-layouts, local_step(): return (q1, q2, loss[0, 0], dz1, dz2, dzs, dcp[:KP])  12 us

profile of v1, /device:TPU:0, one launch (start us, length us, event | category | flops | bytes accessed | tf_op | source)
XLA Modules:
  0.0 141.4 jit_solution(274613183201058478)
XLA Ops:
  0.6 0.7 convert_element_type.3
  1.3 0.1 broadcast_in_dim.14
  1.4 0.6 fusion.3.m8
  2.0 39.5 %sinkhorn.1 = (bf16[8,512,128]{2,1,0:T(8,128)(2,1)}, f32[8,512]{1,0:T(8,128)}, f32[8,512]{1,0:T(8,128)}, f32[16,2,1920]{2,1,0:T(2,128)}, f32[8,128]{1,0:T(8,128)}) custom-call(bf16[32,128]{1,0:T(8,128)(2,1)} %z1.5, bf16[32,128]{1,0:T(8,128)(2,1)} %z2.5, bf16[6,32,128]{2,1,0:T(8,128)(2,1)} %zs.3, f32[8,128]{1,0:T(8,128)} %fusion.3.m8, bf16[30000,128]{1,0:T(8,128)(2,1)} %protos.3), custom_call_target="tpu_custom_call" | custom-call | tf_op jit(solution)/shard_map/sinkhorn/pallas_call | solution.py:454
  41.5 70.7 %grads.1 = (f32[30720,128]{1,0:T(8,128)}, f32[32,128]{1,0:T(8,128)}, f32[32,128]{1,0:T(8,128)}, f32[6,32,128]{2,1,0:T(8,128)}, f32[8,128]{1,0:T(8,128)}) custom-call(bf16[8,512,128]{2,1,0:T(8,128)(2,1)} %get-tuple-element.23.zall, f32[8,512]{1,0:T(8,128)} %get-tuple-element.24.arow, f32[8,512]{1,0:T(8,128)} %get-tuple-element.19.brow, ...), custom_call_target="tpu_custom_call" | custom-call | tf_op jit(solution)/shard_map/grads/pallas_call | solution.py:468
  112.2 0.0 copy-start.1
  112.3 10.8 %slice.7 = f32[30000,128]{1,0:T(8,128)} slice(f32[30720,128]{1,0:T(8,128)} %get-tuple-element.30), slice={[0:30000], [0:128]} | slice | bytes 30720000 | tf_op jit(solution)/shard_map/slice | solution.py:496
  123.1 0.0 copy-start.3
  123.1 0.0 copy-start.2
  123.1 0.0 copy-start
  123.1 1.2 slice.6
  124.3 0.0 copy-done.1
  124.3 0.1 copy.12
  124.4 0.7 dynamic-slice_bitcast_fusion.bcol
  125.1 14.4 %codes.1 = (f32[32,30000]{1,0:T(8,128)}, f32[32,30000]{1,0:T(8,128)}) custom-call(bf16[32,128]{1,0:T(8,128)(2,1)} %z1.5, bf16[32,128]{1,0:T(8,128)(2,1)} %z2.5, f32[32,2]{1,0:T(8,128)} %dynamic-slice_bitcast_fusion.bcol, bf16[30000,128]{1,0:T(8,128)(2,1)} %protos.3, f32[2,30720]{1,0:T(2,128)} %bitcast.6), custom_call_target="tpu_custom_call" | custom-call | tf_op jit(solution)/shard_map/codes/pallas_call | solution.py:485
  139.5 0.0 copy-done.3
  139.5 0.6 copy.16
  140.1 0.0 copy-done.2
  140.1 0.6 copy.17
  140.7 0.0 copy-done
  140.7 0.6 copy.18
  (1 shorter events, 0.0 us)
Async XLA Ops:
  112.2 12.0 %copy-start.1 = (f32[8,512]{1,0:T(8,128)S(1)}, f32[8,512]{1,0:T(8,128)}, u32[]{:S(2)}) copy-start(f32[8,512]{1,0:T(8,128)} %get-tuple-element.19.brow) | copy-start | bytes 49156
  123.1 16.5 %copy-start.3 = (f32[32,128]{1,0:T(8,128)S(1)}, f32[32,128]{1,0:T(8,128)}, u32[]{:S(2)}) copy-start(f32[32,128]{1,0:T(8,128)} %get-tuple-element.41) | copy-start | bytes 49156
  123.1 17.1 %copy-start.2 = (f32[32,128]{1,0:T(8,128)S(1)}, f32[32,128]{1,0:T(8,128)}, u32[]{:S(2)}) copy-start(f32[32,128]{1,0:T(8,128)} %get-tuple-element.42) | copy-start | bytes 49156
  123.1 17.7 %copy-start = (f32[6,32,128]{2,1,0:T(8,128)S(1)}, f32[6,32,128]{2,1,0:T(8,128)}, u32[]{:S(2)}) copy-start(f32[6,32,128]{2,1,0:T(8,128)} %get-tuple-element.43) | copy-start | bytes 294916

commit v2 on v0

v2 whole, which is shorter than its diff:
```python
import jax
import jax.numpy as jnp
from jax import lax
from jax.experimental import pallas as pl
from jax.experimental.pallas import tpu as pltpu
from jax.sharding import PartitionSpec as P

TAU = 0.1
LOG2E = 1.4426950408889634
LN2 = 0.6931471805599453
SCALE = LOG2E / TAU
NDEV = 16
ROWS = 32
NS = 512
VIEWS = 8
D = 128
KP = 30000
SH = 1920
KPAD = SH * NDEV
LAST = KP - SH * (NDEV - 1)
CB = 384
NCH = SH // CB
PAIRS = 14.0
LOGICAL = pl.DeviceIdType.LOGICAL
VM = 36 * 1024 * 1024
RB = 512
NROW = 15
RPI = KPAD // RB // NROW
LAG2, LAG3 = 3, 7
NIT = 2 * NCH + LAG3
STEPS = 2 * NCH


def dot_nt(a, b):
    return lax.dot_general(a, b, (((1,), (1,)), ((), ())), preferred_element_type=jnp.float32)


def dot_nn(a, b):
    return lax.dot_general(a, b, (((1,), (0,)), ((), ())), preferred_element_type=jnp.float32)


def fold8(x):
    return jnp.sum(x.reshape(x.shape[0] // 8, 8, x.shape[1]), axis=0)


def flip(me, bit):
    return me + bit - 2 * bit * lax.rem(me // bit, 2)


def full_barrier(me):
    barrier = pltpu.get_barrier_semaphore()
    for d in range(1, NDEV):
        pl.semaphore_signal(barrier, inc=1, device_id=lax.rem(me + d, NDEV), device_id_type=LOGICAL)
    pl.semaphore_wait(barrier, NDEV - 1)


def send(src, dst, ssem, rsem, to):
    copy = pltpu.make_async_remote_copy(src_ref=src, dst_ref=dst, send_sem=ssem, recv_sem=rsem,
                                        device_id=to, device_id_type=LOGICAL)
    copy.start()


def drain(ref, sem):
    pltpu.make_async_copy(ref, ref, sem).wait()


def kernel(z1, z2, zs, mpad, protos, dc, q1, q2, dz, loss,
           ca, ex, slots, lslots, wall, zall, arow, brow, gt, zl, cols, acc,
           csem, zsend, zlrecv, zs1recv, zs2send, zs2recv, arsend, arrecv, lsend, lrecv, wsend, wrecv,
           ssem, r2, r3, rs):
    me = lax.axis_index("data")
    cc = pltpu.make_async_copy(protos, ca.at[pl.ds(0, KP)], csem)
    cc.start()
    ca[pl.ds(KP, KPAD - KP), :] = jnp.zeros((KPAD - KP, D), jnp.bfloat16)
    dims = (flip(me, 2), flip(me, 4), flip(me, 8))
    sib = flip(me, 1)
    here = lax.broadcasted_iota(jnp.int32, (8, 128), 0) == me // 4
    slots[0, me] = jnp.where(here, pltpu.roll(mpad[...], ROWS * lax.rem(me, 4), 1), 0.0)
    with jax.named_scope("barrier"):
        full_barrier(me)
    myrows = pl.ds(pl.multiple_of(me * ROWS, ROWS), ROWS)

    def ar_send(t):
        for d in range(1, NDEV):
            send(slots.at[t, me], slots.at[t, me], arsend.at[t], arrecv.at[t], lax.rem(me + d, NDEV))

    def ar_total(t):
        drain(slots.at[t, pl.ds(0, NDEV - 1)], arrecv.at[t])
        tot = slots[t, 0]
        for i in range(1, NDEV):
            tot = tot + slots[t, i]
        return tot

    for d in range(1, NDEV):
        to = lax.rem(me + d, NDEV)
        send(z1, zall.at[0, myrows], zsend.at[0], zlrecv, to)
        send(z2, zall.at[1, myrows], zsend.at[0], zlrecv, to)
    ar_send(0)
    for d in range(1, NDEV // 2):
        send(zs, zall.at[pl.ds(2, 6), myrows], zsend.at[1], zs1recv, lax.rem(me + 2 * d, NDEV))
    zall[0, myrows] = z1[...]
    zall[1, myrows] = z2[...]
    zall[pl.ds(2, 6), myrows] = zs[...]
    send(zs, zall.at[pl.ds(2, 6), myrows], zs2send, zs2recv, sib)
    zl[pl.ds(0, ROWS)] = z1[...]
    zl[pl.ds(ROWS, ROWS)] = z2[...]
    zl[pl.ds(2 * ROWS, 6 * ROWS)] = zs[...].reshape(6 * ROWS, D)
    acc[...] = jnp.zeros_like(acc)
    cc.wait()
    with jax.named_scope("mask"):
        mask8 = ar_total(0)
    live = jnp.sum(jnp.sum(mask8, axis=1, keepdims=True), axis=0, keepdims=True)
    mrow = jnp.concatenate([mask8[j:j + 1] for j in range(4)], axis=1)
    with jax.named_scope("zlarge"):
        drain(zall.at[pl.ds(0, 2), pl.ds(0, NS - ROWS)], zlrecv)

    def shard(b):
        return ca[pl.ds(pl.multiple_of(me * SH + b * CB, 128), CB)]

    def col_scale(c, b):
        k = me * SH + b * CB + lax.broadcasted_iota(jnp.int32, (CB, 1), 0)
        return jnp.where(k < KP, 1.0 / (KP * c), 0.0)

    zero8 = jnp.zeros((8, NS), jnp.float32)

    def first(b, carry):
        rows = pl.ds(pl.multiple_of(b * CB, CB), CB)
        out = []
        for v in range(2):
            ps, r = carry[2 * v], carry[2 * v + 1]
            p = jnp.exp2(dot_nt(shard(b), zall[v]) * SCALE)
            ps = ps + fold8(p)
            e = p * p * mrow
            ex[v, rows] = e
            w = col_scale(jnp.sum(e, axis=1, keepdims=True), b)
            r = r + fold8(e * w)
            out += [ps, r]
        return tuple(out)

    def put(t, r1, r2):
        for v, r in enumerate((r1, r2)):
            row = jnp.sum(r, axis=0, keepdims=True)
            for j in range(4):
                slots[t, me, pl.ds(4 * v + j, 1)] = row[:, 128 * j:128 * (j + 1)]

    def scale_rows(tot):
        us = []
        for v in range(2):
            r = jnp.concatenate([tot[4 * v + j:4 * v + j + 1] for j in range(4)], axis=1)
            us.append(mrow / (live * jnp.where(mrow > 0, r, 1.0)))
        return us

    pad = jnp.where(me == NDEV - 1, float(SH - LAST), 0.0)

    def put_lse(v, ps):
        row = jnp.sum(ps, axis=0, keepdims=True) - pad
        for j in range(4):
            lslots[me, pl.ds(4 * v + j, 1)] = row[:, 128 * j:128 * (j + 1)]

    with jax.named_scope("first"):
        ps1, r1, ps2, rr2 = lax.fori_loop(0, NCH, first, (zero8, zero8, zero8, zero8))
        put(1, r1, rr2)
        ar_send(1)
    put_lse(0, ps1)
    put_lse(1, ps2)
    with jax.named_scope("zsmall1"):
        drain(zall.at[pl.ds(2, 6), pl.ds(0, 7 * ROWS)], zs1recv)
    for d in range(1, NDEV // 2):
        rows = pl.ds(pl.multiple_of(lax.rem(me + 2 * d, NDEV) * ROWS, ROWS), ROWS)
        send(zall.at[pl.ds(2, 6), rows], zall.at[pl.ds(2, 6), rows], zs2send, zs2recv, sib)
    with jax.named_scope("ar1"):
        us = scale_rows(ar_total(1))

    def again(us, last):
        def step(b, carry):
            rows = pl.ds(pl.multiple_of(b * CB, CB), CB)
            out = []
            for v in range(2):
                e = ex[v, rows]
                w = col_scale(jnp.sum(e * us[v], axis=1, keepdims=True), b)
                out.append(carry[v] + fold8(e * w))
                if last:
                    for q in range(CB // 128):
                        wt = jnp.broadcast_to(w[128 * q:128 * (q + 1)], (128, 128)).T
                        wall[me, pl.ds(v, 1), pl.ds(pl.multiple_of(b * CB + 128 * q, 128), 128)] = wt[0:1]
            return tuple(out)
        return step

    with jax.named_scope("again2"):
        r1, rr2 = lax.fori_loop(0, NCH, again(us, False), (zero8, zero8))
        put(2, r1, rr2)
        ar_send(2)
    with jax.named_scope("zsmall2"):
        drain(zall.at[pl.ds(2, 6), pl.ds(0, 8 * ROWS)], zs2recv)

    def small(i, carry):
        v = 2 + i

        def blk(b, ps):
            return ps + fold8(jnp.exp2(dot_nt(shard(b), zall[v]) * SCALE))

        put_lse(v, lax.fori_loop(0, NCH, blk, zero8))
        return carry

    with jax.named_scope("small"):
        lax.fori_loop(0, 6, small, 0)
        for d in range(1, NDEV):
            send(lslots.at[me], lslots.at[me], lsend, lrecv, lax.rem(me + d, NDEV))
    with jax.named_scope("ar2"):
        us = scale_rows(ar_total(2))
    with jax.named_scope("again3"):
        r1, rr2 = lax.fori_loop(0, NCH, again(us, True), (zero8, zero8))
        put(3, r1, rr2)
        ar_send(3)
        for d in range(1, NDEV):
            send(wall.at[me], wall.at[me], wsend, wrecv, lax.rem(me + d, NDEV))
    gsc = 1.0 / (TAU * PAIRS * live)
    with jax.named_scope("lse"):
        drain(lslots.at[pl.ds(0, NDEV - 1)], lrecv)
        tot = lslots[0]
        for i in range(1, NDEV):
            tot = tot + lslots[i]
        inv = 1.0 / tot
        for v in range(VIEWS):
            for j in range(4):
                coef = 1.0 if v < 2 else 2.0
                arow[v:v + 1, 128 * j:128 * (j + 1)] = (coef * gsc) * (mask8[j:j + 1] * inv[4 * v + j:4 * v + j + 1])
        weight = jnp.concatenate([mask8[0:4]] * 2 + [2.0 * mask8[0:4]] * 6, axis=0)
        lsum = jnp.sum(jnp.sum(weight * jnp.log(tot), axis=1, keepdims=True), axis=0, keepdims=True)
    with jax.named_scope("ar3"):
        us = scale_rows(ar_total(3))
    for v in range(2):
        brow[v:v + 1] = live * us[v]
    brow[2:8] = jnp.zeros((6, NS), jnp.float32)
    tile = pl.ds(pl.multiple_of((me // 4) * 128, 128), 128)
    cols[0] = arow[:, tile].T
    cols[1] = brow[:, tile].T
    mine = pl.ds(pl.multiple_of(lax.rem(me, 4) * ROWS, ROWS), ROWS)

    def piece_row(owner, t, a):
        return pl.multiple_of(owner * SH + t * CB + a * 128, 128)

    def push(owner, it, a, to, rsem):
        ref = dc.at[pl.ds(piece_row(owner, it // 2, a), 128)]
        send(ref, ref, ssem.at[it, a], rsem.at[it, a], to)

    def order(a):
        return dims[a], dims[(a + 1) % 3], dims[(a + 2) % 3]

    def owner_of(holder, d0, it):
        return holder + lax.rem(it, 2) * (d0 - me)

    def chunk(it):
        t = it // 2
        owners = [owner_of(me, dims[a], it) for a in range(3)]
        c = jnp.concatenate([ca[pl.ds(piece_row(owners[a], t, a), 128)] for a in range(3)], axis=0)
        wc = []
        for v in range(2):
            parts = []
            for a in range(3):
                off = pl.multiple_of(t * CB + a * 128, 128)
                row = wall[owners[a], pl.ds(v, 1), pl.ds(off, 128)] * gsc
                parts.append(jnp.broadcast_to(row, (128, 128)).T)
            wc.append(jnp.concatenate(parts, axis=0))

        def nblk(nb, carry):
            ln = pl.ds(pl.multiple_of(nb * 256, 256), 256)
            s = [dot_nt(c, zall[v, ln]) for v in range(VIEWS)]
            av = [arow[v:v + 1, ln] for v in range(VIEWS)]
            bv = [brow[v:v + 1, ln] for v in range(2)]
            for q in range(CB // 64):
                sl = slice(64 * q, 64 * (q + 1))
                w0 = jnp.concatenate([wc[0][sl], wc[0][sl]], axis=1)
                w1 = jnp.concatenate([wc[1][sl], wc[1][sl]], axis=1)
                p0 = jnp.exp2(s[0][sl] * SCALE)
                p1 = jnp.exp2(s[1][sl] * SCALE)
                x0 = (p0 * p0) * bv[0] * w0
                x1 = (p1 * p1) * bv[1] * w1
                xs = x0 + x1
                gs = [p0 * av[0] - x1, p1 * av[1] - x0]
                for v in range(2, VIEWS):
                    gs.append(jnp.exp2(s[v][sl] * SCALE) * av[v] - xs)
                for v in range(VIEWS):
                    gt[pl.ds(64 * q, 64), pl.ds(pl.multiple_of(v * NS + nb * 256, 256), 256)] = gs[v].astype(jnp.bfloat16)
            return carry

        lax.fori_loop(0, 2, nblk, 0)
        res = dot_nn(gt[...], zall[...].reshape(VIEWS * NS, D))
        for a in range(3):
            dc[pl.ds(piece_row(owners[a], t, a), 128)] = res[128 * a:128 * (a + 1)]

    def rows_part(i):
        ac = cols[0, mine]
        bc = cols[1, mine]
        for h in range(RPI):
            jb = i * RPI + h
            c = ca[pl.ds(pl.multiple_of(jb * RB, RB), RB)]
            s = dot_nt(zl[...], c) * SCALE
            wr = []
            for v in range(2):
                parts = []
                for q in range(RB // 128):
                    b = jb * (RB // 128) + q
                    parts.append(wall[b // (SH // 128), pl.ds(v, 1), pl.ds(pl.multiple_of(lax.rem(b, SH // 128) * 128, 128), 128)])
                wr.append(jnp.concatenate(parts, axis=1))
            sv = [s[ROWS * v:ROWS * (v + 1)] for v in range(VIEWS)]
            p0 = jnp.exp2(sv[0])
            p1 = jnp.exp2(sv[1])
            o0 = (p0 * p0) * bc[:, 0:1] * wr[0]
            o1 = (p1 * p1) * bc[:, 1:2] * wr[1]

            q1[:, pl.ds(pl.multiple_of(jb * RB, RB), RB)] = o0
            q2[:, pl.ds(pl.multiple_of(jb * RB, RB), RB)] = o1
            x0 = o0 * gsc
            x1 = o1 * gsc
            xs = x0 + x1
            gs = [p0 * ac[:, 0:1] - x1, p1 * ac[:, 1:2] - x0]
            ssum = sv[2]
            for v in range(3, VIEWS):
                ssum = ssum + sv[v]
            for v in range(2, VIEWS):
                gs.append(jnp.exp2(sv[v]) * ac[:, v:v + 1] - xs)
            g = jnp.concatenate([x.astype(jnp.bfloat16) for x in gs], axis=0)
            acc[pl.ds(0, VIEWS * ROWS)] += dot_nn(g, c)
            ls = x1 * sv[0] + x0 * sv[1] + xs * ssum
            part = ls[:, 0:128]
            for q in range(1, RB // 128):
                part = part + ls[:, 128 * q:128 * (q + 1)]
            acc[pl.ds(VIEWS * ROWS, ROWS)] += part

    def own(it):
        for a in range(3):
            d0, d1, d2 = order(a)
            o = owner_of(me, d0, it)
            push(o, it, a, d1, r2)
            push(o, it, a, d2, r3)
            push(o, it, a, sib, rs)

    def serve2(it):
        for a in range(3):
            d0, d1, d2 = order(a)
            drain(dc.at[pl.ds(0, 128)], r2.at[it, a])
            o = owner_of(d1, d0, it)
            push(o, it, a, d2, r3)
            push(o, it, a, sib, rs)

    def serve3(it):
        for a in range(3):
            d0, d1, d2 = order(a)
            drain(dc.at[pl.ds(0, 256)], r3.at[it, a])
            for holder in (d2, d2 + d1 - me):
                push(owner_of(holder, d0, it), it, a, sib, rs)

    def main(it, carry):
        @pl.when(it < STEPS)
        def _():
            with jax.named_scope("chunk"):
                chunk(it)
            own(it)

        @pl.when(it == 0)
        def _():
            with jax.named_scope("wait_w"):
                drain(wall.at[pl.ds(0, NDEV - 1)], wrecv)

        @pl.when(jnp.logical_and(it >= LAG2, it < LAG2 + STEPS))
        def _():
            with jax.named_scope("serve2"):
                serve2(it - LAG2)

        @pl.when(it < NROW)
        def _():
            with jax.named_scope("rows"):
                rows_part(it)

        @pl.when(it >= LAG3)
        def _():
            with jax.named_scope("serve3"):
                serve3(it - LAG3)

        return carry

    lax.fori_loop(0, NIT, main, 0)

    total = jnp.sum(jnp.sum(acc[pl.ds(VIEWS * ROWS, ROWS)], axis=1, keepdims=True), axis=0, keepdims=True)
    slots[4, me] = jnp.broadcast_to(total, (8, 128))
    ar_send(4)
    dz[...] = acc[pl.ds(0, VIEWS * ROWS)].reshape(VIEWS, ROWS, D)
    with jax.named_scope("loss"):
        tot = ar_total(4)
    cross = tot[0:1, 0:1] * (LN2 * TAU * PAIRS) * live - lsum
    loss[...] = jnp.broadcast_to(-cross / (live * PAIRS), (8, 128))

    def finish(it, carry):
        for a in range(3):
            drain(dc.at[pl.ds(0, 4 * 128)], rs.at[it, a])
            drain(dc.at[pl.ds(0, 7 * 128)], ssem.at[it, a])
        return carry

    with jax.named_scope("finish"):
        lax.fori_loop(0, STEPS, finish, 0)
    drain(zall.at[pl.ds(0, 2), pl.ds(0, NS - ROWS)], zsend.at[0])
    drain(zall.at[pl.ds(2, 6), pl.ds(0, 7 * ROWS)], zsend.at[1])
    drain(zall.at[pl.ds(2, 6), pl.ds(0, 8 * ROWS)], zs2send)
    for t in range(5):
        drain(slots.at[t, pl.ds(0, NDEV - 1)], arsend.at[t])
    drain(lslots.at[pl.ds(0, NDEV - 1)], lsend)
    drain(wall.at[pl.ds(0, NDEV - 1)], wsend)


def local_step(z_one, z_two, z_small, protos, live_mask):
    mpad = jnp.broadcast_to(jnp.pad(live_mask.astype(jnp.float32), (0, 128 - ROWS))[None, :], (8, 128))
    f32 = jnp.float32
    bf16 = jnp.bfloat16
    vmem = pl.BlockSpec(memory_space=pltpu.VMEM)
    anym = pl.BlockSpec(memory_space=pl.ANY)
    dma = pltpu.SemaphoreType.DMA
    vm = pltpu.VMEM
    dc, q1, q2, dz, loss = pl.pallas_call(
        kernel,
        out_shape=[vm((KPAD, D), f32), vm((ROWS, KPAD), f32), vm((ROWS, KPAD), f32),
                   vm((VIEWS, ROWS, D), f32), vm((8, 128), f32)],
        in_specs=[vmem] * 4 + [anym],
        out_specs=[vmem] * 5,
        scratch_shapes=[vm((KPAD, D), bf16), vm((2, SH, NS), f32), vm((5, NDEV, 8, 128), f32), vm((NDEV, 32, 128), f32),
                        vm((NDEV, 2, SH), f32), vm((VIEWS, NS, D), bf16), vm((8, NS), f32), vm((8, NS), f32),
                        vm((CB, VIEWS * NS), bf16), vm((VIEWS * ROWS, D), bf16), vm((2, 128, 8), f32),
                        vm((VIEWS * ROWS + ROWS, D), f32),
                        dma, dma((2,)), dma, dma, dma, dma, dma((5,)), dma((5,)), dma, dma, dma, dma,
                        dma((STEPS, 3)), dma((STEPS, 3)), dma((STEPS, 3)), dma((STEPS, 3))],
        compiler_params=pltpu.CompilerParams(collective_id=0, has_side_effects=True, vmem_limit_bytes=VM),
        name="step",
    )(z_one, z_two, z_small, mpad, protos)
    return q1[:, :KP], q2[:, :KP], loss[0, 0], dz[0], dz[1], dz[2:], dc[:KP]


def solution(mesh):
    row_spec = P("data", None)
    crop_spec = P(None, "data", None)
    return jax.shard_map(local_step, mesh=mesh,
                         in_specs=(row_spec, row_spec, crop_spec, P(None, None), P("data")),
                         out_specs=(row_spec, row_spec, P(), row_spec, row_spec, crop_spec, P(None, None)),
                         check_vma=False)
```

time: 690 us -> 108 us (0.16)
  waiting for transfers between devices: 428 us -> 0 us
  Pallas kernels: 0 us -> 93.8 us
  matrix products: 81 us -> 0 us
  other arithmetic: 75 us -> 0.66 us
  blocking collectives: 66.6 us -> 0 us
  between operations: 19.5 us -> 0.64 us
    psum x7 -> x0, waiting for transfers between devices: 427 us -> none  [the longest x6 315 us: value_a14(): col_sum = lax.psum(jnp.sum(weights, axis=0), 'data')]
    pallas_call x0 -> x1, Pallas kernels: none -> 93.8 us  [local_step(): pl.pallas_call(kernel, out_shape=[vm((KPAD, D), f32), vm((ROWS, KPAD), f3...]
    dot_general x9 -> x0, matrix products: 81 us -> none  [the longest x1 16.9 us: loss_and_grads(): jnp.einsum('nk,nd->kd', grad_two, z_two, preferred_element_type=jnp.float32)]
    psum x2 -> x0, blocking collectives: 66.6 us -> none  [the longest x1 34.7 us: local_step(): live_total = lax.psum(jnp.sum(live_f), 'data')]
    reduce_sum x14 -> x0, other arithmetic: 39.9 us -> none  [the longest x6 17.1 us: value_a14(): row_sum = jnp.sum(weights, axis=1, keepdims=True)]
    convert_element_type x4 -> x1, other arithmetic: 22.3 us -> 0.66 us  [local_step(): live_mask.astype(jnp.float32)]
    unnamed x35 -> x0, local copies, waits for them, and re-layouts: 18.3 us -> none
    slice x0 -> x5, local copies, waits for them, and re-layouts: none -> 11.3 us  [local_step(): return (q1[:, :KP], q2[:, :KP], loss[0, 0], dz[0], dz[1], dz[2:], dc[:KP])]
  transfers between devices with their start and end apart: 7 -> 0, of which waited for: 7 -> 0; matrix products, arithmetic and copies ran while one was open for 8% -> 0% of each run, Pallas kernels for 0% -> 0%
where the time goes in v2:
time: 108 us
  Pallas kernels  93.8 us (87%)
  local copies, waits for them, and re-layouts  12.5 us (12%)
    pallas_call x1, Pallas kernels, local_step(): pl.pallas_call(kernel, out_shape=[vm((KPAD, D), f32), vm((ROWS, KPAD), f3...  93.8 us
    slice x5, local copies, waits for them, and re-layouts, local_step(): return (q1[:, :KP], q2[:, :KP], loss[0, 0], dz[0], dz[1], dz[2:], dc[:KP])  11.3 us

profile of v2, /device:TPU:0, one launch (start us, length us, event | category | flops | bytes accessed | tf_op | source)
XLA Modules:
  0.0 107.6 jit_solution(13442316993913903558)
XLA Ops:
  0.6 0.7 convert_element_type.5
  1.3 0.6 broadcast_in_dim.2.mpad
  1.9 93.8 %step.1 = (f32[30720,128]{1,0:T(8,128)S(1)}, f32[32,30720]{1,0:T(8,128)S(1)}, f32[32,30720]{1,0:T(8,128)S(1)}, f32[8,32,128]{2,1,0:T(8,128)S(1)}, f32[8,128]{1,0:T(8,128)S(1)}) custom-call(bf16[32,128]{1,0:T(8,128)(2,1)} %z1.1, bf16[32,128]{1,0:T(8,128)(2,1)} %z2.1, bf16[6,32,128]{2,1,0:T(8,128)(2,1)} %zs.1, f32[8,128]{1,0:T(8,128)} %broadcast_in_dim.2.mpad, ...), custom_call_target="tpu_custom_call" | custom-call | tf_op jit(solution)/shard_map/step/pallas_call | solution.py:419
  95.7 0.5 slice.23
  96.2 2.1 %slice.21 = f32[32,30000]{1,0:T(8,128)} slice(f32[32,30720]{1,0:T(8,128)S(1)} %get-tuple-element.12), slice={[0:32], [0:30000]} | slice | bytes 7680000 | tf_op jit(solution)/shard_map/slice | solution.py:434
  98.3 0.6 slice_bitcast_fusion
  99.0 0.6 slice.26
  99.6 2.1 %slice.22 = f32[32,30000]{1,0:T(8,128)} slice(f32[32,30720]{1,0:T(8,128)S(1)} %get-tuple-element.13), slice={[0:32], [0:30000]} | slice | bytes 7680000 | tf_op jit(solution)/shard_map/slice | solution.py:434
  101.8 5.8 %slice.27 = f32[30000,128]{1,0:T(8,128)} slice(f32[30720,128]{1,0:T(8,128)S(1)} %get-tuple-element.16), slice={[0:30000], [0:128]} | slice | bytes 30720000 | tf_op jit(solution)/shard_map/slice | solution.py:434
  (1 shorter events, 0.0 us)

commit v3 on v2

--- a/solution.py
+++ b/solution.py
@@ -64,7 +64,7 @@
     pltpu.make_async_copy(ref, ref, sem).wait()
 
 
-def kernel(z1, z2, zs, mpad, protos, dc, q1, q2, dz, loss,
+def kernel(z1, z2, zs, mask, protos, dc, q1, q2, dz, loss,
            ca, ex, slots, lslots, wall, zall, arow, brow, gt, zl, cols, acc,
            csem, zsend, zlrecv, zs1recv, zs2send, zs2recv, arsend, arrecv, lsend, lrecv, wsend, wrecv,
            ssem, r2, r3, rs):
@@ -75,7 +75,8 @@
     dims = (flip(me, 2), flip(me, 4), flip(me, 8))
     sib = flip(me, 1)
     here = lax.broadcasted_iota(jnp.int32, (8, 128), 0) == me // 4
-    slots[0, me] = jnp.where(here, pltpu.roll(mpad[...], ROWS * lax.rem(me, 4), 1), 0.0)
+    mpad = jnp.concatenate([mask[...].astype(jnp.float32), jnp.zeros((1, 128 - ROWS), jnp.float32)], axis=1)
+    slots[0, me] = jnp.where(here, pltpu.roll(jnp.broadcast_to(mpad, (8, 128)), ROWS * lax.rem(me, 4), 1), 0.0)
     with jax.named_scope("barrier"):
         full_barrier(me)
     myrows = pl.ds(pl.multiple_of(me * ROWS, ROWS), ROWS)
@@ -124,7 +125,7 @@
     zero8 = jnp.zeros((8, NS), jnp.float32)
 
     def first(b, carry):
-        rows = pl.ds(pl.multiple_of(b * CB, CB), CB)
+        rows = pl.ds(b * CB, CB)
         out = []
         for v in range(2):
             ps, r = carry[2 * v], carry[2 * v + 1]
@@ -158,7 +159,10 @@
             lslots[me, pl.ds(4 * v + j, 1)] = row[:, 128 * j:128 * (j + 1)]
 
     with jax.named_scope("first"):
-        ps1, r1, ps2, rr2 = lax.fori_loop(0, NCH, first, (zero8, zero8, zero8, zero8))
+        carry = (zero8,) * 4
+        for b in range(NCH):
+            carry = first(b, carry)
+        ps1, r1, ps2, rr2 = carry
         put(1, r1, rr2)
         ar_send(1)
     put_lse(0, ps1)
@@ -168,6 +172,19 @@
     for d in range(1, NDEV // 2):
         rows = pl.ds(pl.multiple_of(lax.rem(me + 2 * d, NDEV) * ROWS, ROWS), ROWS)
         send(zall.at[pl.ds(2, 6), rows], zall.at[pl.ds(2, 6), rows], zs2send, zs2recv, sib)
+    def small(i, carry):
+        v = 2 + i
+        ps = zero8
+        for b in range(NCH):
+            ps = ps + fold8(jnp.exp2(dot_nt(shard(b), zall[v]) * SCALE))
+        put_lse(v, ps)
+        return carry
+
+    with jax.named_scope("zsmall2"):
+        drain(zall.at[pl.ds(2, 6), pl.ds(0, 8 * ROWS)], zs2recv)
+
+    with jax.named_scope("small"):
+        lax.fori_loop(0, 3, small, 0)
     with jax.named_scope("ar1"):
         us = scale_rows(ar_total(1))
 
@@ -190,20 +207,8 @@
         r1, rr2 = lax.fori_loop(0, NCH, again(us, False), (zero8, zero8))
         put(2, r1, rr2)
         ar_send(2)
-    with jax.named_scope("zsmall2"):
-        drain(zall.at[pl.ds(2, 6), pl.ds(0, 8 * ROWS)], zs2recv)
-
-    def small(i, carry):
-        v = 2 + i
-
-        def blk(b, ps):
-            return ps + fold8(jnp.exp2(dot_nt(shard(b), zall[v]) * SCALE))
-
-        put_lse(v, lax.fori_loop(0, NCH, blk, zero8))
-        return carry
-
     with jax.named_scope("small"):
-        lax.fori_loop(0, 6, small, 0)
+        lax.fori_loop(3, 6, small, 0)
         for d in range(1, NDEV):
             send(lslots.at[me], lslots.at[me], lsend, lrecv, lax.rem(me + d, NDEV))
     with jax.named_scope("ar2"):
@@ -263,8 +268,8 @@
                 parts.append(jnp.broadcast_to(row, (128, 128)).T)
             wc.append(jnp.concatenate(parts, axis=0))
 
-        def nblk(nb, carry):
-            ln = pl.ds(pl.multiple_of(nb * 256, 256), 256)
+        def nblk(nb):
+            ln = pl.ds(nb * 256, 256)
             s = [dot_nt(c, zall[v, ln]) for v in range(VIEWS)]
             av = [arow[v:v + 1, ln] for v in range(VIEWS)]
             bv = [brow[v:v + 1, ln] for v in range(2)]
@@ -281,17 +286,19 @@
                 for v in range(2, VIEWS):
                     gs.append(jnp.exp2(s[v][sl] * SCALE) * av[v] - xs)
                 for v in range(VIEWS):
-                    gt[pl.ds(64 * q, 64), pl.ds(pl.multiple_of(v * NS + nb * 256, 256), 256)] = gs[v].astype(jnp.bfloat16)
-            return carry
-
-        lax.fori_loop(0, 2, nblk, 0)
-        res = dot_nn(gt[...], zall[...].reshape(VIEWS * NS, D))
+                    gt[nb, pl.ds(64 * q, 64), pl.ds(v * 256, 256)] = gs[v].astype(jnp.bfloat16)
+            zz = jnp.concatenate([zall[v, ln] for v in range(VIEWS)], axis=0)
+            return dot_nn(gt[nb], zz)
+
+        res = nblk(0)
+        res = res + nblk(1)
         for a in range(3):
             dc[pl.ds(piece_row(owners[a], t, a), 128)] = res[128 * a:128 * (a + 1)]
 
     def rows_part(i):
         ac = cols[0, mine]
         bc = cols[1, mine]
+        outs = []
         for h in range(RPI):
             jb = i * RPI + h
             c = ca[pl.ds(pl.multiple_of(jb * RB, RB), RB)]
@@ -309,8 +316,7 @@
             o0 = (p0 * p0) * bc[:, 0:1] * wr[0]
             o1 = (p1 * p1) * bc[:, 1:2] * wr[1]
 
-            q1[:, pl.ds(pl.multiple_of(jb * RB, RB), RB)] = o0
-            q2[:, pl.ds(pl.multiple_of(jb * RB, RB), RB)] = o1
+            outs.append((o0, o1))
             x0 = o0 * gsc
             x1 = o1 * gsc
             xs = x0 + x1
@@ -328,6 +334,22 @@
                 part = part + ls[:, 128 * q:128 * (q + 1)]
             acc[pl.ds(VIEWS * ROWS, ROWS)] += part
 
+        @pl.when(i < NROW - 1)
+        def _():
+            for h in range(RPI):
+                ln = pl.ds(pl.multiple_of((i * RPI + h) * RB, RB), RB)
+                q1[:, ln] = outs[h][0]
+                q2[:, ln] = outs[h][1]
+
+        @pl.when(i == NROW - 1)
+        def _():
+            for h in range(RPI):
+                lo = ((NROW - 1) * RPI + h) * RB
+                n = min(RB, KP - lo)
+                if n > 0:
+                    q1[:, pl.ds(lo, n)] = outs[h][0][:, :n]
+                    q2[:, pl.ds(lo, n)] = outs[h][1][:, :n]
+
     def own(it):
         for a in range(3):
             d0, d1, d2 = order(a)
@@ -373,6 +395,12 @@
             with jax.named_scope("rows"):
                 rows_part(it)
 
+        @pl.when(it == NROW)
+        def _():
+            total = jnp.sum(jnp.sum(acc[pl.ds(VIEWS * ROWS, ROWS)], axis=1, keepdims=True), axis=0, keepdims=True)
+            slots[4, me] = jnp.broadcast_to(total, (8, 128))
+            ar_send(4)
+
         @pl.when(it >= LAG3)
         def _():
             with jax.named_scope("serve3"):
@@ -382,14 +410,11 @@
 
     lax.fori_loop(0, NIT, main, 0)
 
-    total = jnp.sum(jnp.sum(acc[pl.ds(VIEWS * ROWS, ROWS)], axis=1, keepdims=True), axis=0, keepdims=True)
-    slots[4, me] = jnp.broadcast_to(total, (8, 128))
-    ar_send(4)
     dz[...] = acc[pl.ds(0, VIEWS * ROWS)].reshape(VIEWS, ROWS, D)
     with jax.named_scope("loss"):
         tot = ar_total(4)
     cross = tot[0:1, 0:1] * (LN2 * TAU * PAIRS) * live - lsum
-    loss[...] = jnp.broadcast_to(-cross / (live * PAIRS), (8, 128))
+    loss[...] = -cross / (live * PAIRS)
 
     def finish(it, carry):
         for a in range(3):
@@ -408,8 +433,17 @@
     drain(wall.at[pl.ds(0, NDEV - 1)], wsend)
 
 
+def emit_kernel(dc, q1, q2, dz, loss, o_q1, o_q2, o_loss, o_z1, o_z2, o_zs, o_dc, sem):
+    pairs = [(dc.at[pl.ds(0, KP)], o_dc), (q1, o_q1), (q2, o_q2), (loss, o_loss),
+             (dz.at[0], o_z1), (dz.at[1], o_z2), (dz.at[pl.ds(2, 6)], o_zs)]
+    copies = [pltpu.make_async_copy(a, b, sem.at[i]) for i, (a, b) in enumerate(pairs)]
+    for c in copies:
+        c.start()
+    for c in copies:
+        c.wait()
+
+
 def local_step(z_one, z_two, z_small, protos, live_mask):
-    mpad = jnp.broadcast_to(jnp.pad(live_mask.astype(jnp.float32), (0, 128 - ROWS))[None, :], (8, 128))
     f32 = jnp.float32
     bf16 = jnp.bfloat16
     vmem = pl.BlockSpec(memory_space=pltpu.VMEM)
@@ -418,20 +452,32 @@
     vm = pltpu.VMEM
     dc, q1, q2, dz, loss = pl.pallas_call(
         kernel,
-        out_shape=[vm((KPAD, D), f32), vm((ROWS, KPAD), f32), vm((ROWS, KPAD), f32),
-                   vm((VIEWS, ROWS, D), f32), vm((8, 128), f32)],
+        out_shape=[vm((KPAD, D), f32), vm((ROWS, KP), f32), vm((ROWS, KP), f32),
+                   vm((VIEWS, ROWS, D), f32), vm((1, 1), f32)],
         in_specs=[vmem] * 4 + [anym],
         out_specs=[vmem] * 5,
         scratch_shapes=[vm((KPAD, D), bf16), vm((2, SH, NS), f32), vm((5, NDEV, 8, 128), f32), vm((NDEV, 32, 128), f32),
                         vm((NDEV, 2, SH), f32), vm((VIEWS, NS, D), bf16), vm((8, NS), f32), vm((8, NS), f32),
-                        vm((CB, VIEWS * NS), bf16), vm((VIEWS * ROWS, D), bf16), vm((2, 128, 8), f32),
+                        vm((2, CB, VIEWS * 256), bf16), vm((VIEWS * ROWS, D), bf16), vm((2, 128, 8), f32),
                         vm((VIEWS * ROWS + ROWS, D), f32),
                         dma, dma((2,)), dma, dma, dma, dma, dma((5,)), dma((5,)), dma, dma, dma, dma,
                         dma((STEPS, 3)), dma((STEPS, 3)), dma((STEPS, 3)), dma((STEPS, 3))],
         compiler_params=pltpu.CompilerParams(collective_id=0, has_side_effects=True, vmem_limit_bytes=VM),
         name="step",
-    )(z_one, z_two, z_small, mpad, protos)
-    return q1[:, :KP], q2[:, :KP], loss[0, 0], dz[0], dz[1], dz[2:], dc[:KP]
+    )(z_one, z_two, z_small, live_mask.reshape(1, ROWS), protos)
+    q1, q2, loss, dz1, dz2, dzs, dc = pl.pallas_call(
+        emit_kernel,
+        out_shape=[jax.ShapeDtypeStruct((ROWS, KP), f32), jax.ShapeDtypeStruct((ROWS, KP), f32),
+                   jax.ShapeDtypeStruct((1, 1), f32), jax.ShapeDtypeStruct((ROWS, D), f32),
+                   jax.ShapeDtypeStruct((ROWS, D), f32), jax.ShapeDtypeStruct((6, ROWS, D), f32),
+                   jax.ShapeDtypeStruct((KP, D), f32)],
+        in_specs=[vmem] * 5,
+        out_specs=[anym] * 7,
+        scratch_shapes=[dma((7,))],
+        compiler_params=pltpu.CompilerParams(vmem_limit_bytes=1024 * 1024),
+        name="emit",
+    )(dc, q1, q2, dz, loss)
+    return q1, q2, loss.reshape(()), dz1, dz2, dzs, dc
 
 
 def solution(mesh):

time: 108 us -> 96.4 us (0.89)
  local copies, waits for them, and re-layouts: 12.5 us -> 0 us
  Pallas kernels: 93.8 us -> 95.6 us
    slice x5 -> x0, local copies, waits for them, and re-layouts: 11.3 us -> none  [local_step(): return (q1[:, :KP], q2[:, :KP], loss[0, 0], dz[0], dz[1], dz[2:], dc[:KP])]
    pallas_call x1 -> x2, Pallas kernels: 93.8 us -> 95.6 us  [the longest x1 86.8 us: local_step(): pl.pallas_call(kernel, out_shape=[vm((KPAD, D), f32), vm((ROWS, KP), f32)...]
where the time goes in v3:
time: 96.4 us; the launch traced here: 96.2 us
  Pallas kernels  95.6 us (99%)
    pallas_call x1, Pallas kernels, local_step(): pl.pallas_call(kernel, out_shape=[vm((KPAD, D), f32), vm((ROWS, KP), f32)...  86.8 us
    pallas_call x1, Pallas kernels, local_step(): pl.pallas_call(emit_kernel, out_shape=[jax.ShapeDtypeStruct((ROWS, KP), f...  8.81 us

profile of v3, /device:TPU:0, one launch (start us, length us, event | category | flops | bytes accessed | tf_op | source)
XLA Modules:
  0.0 96.2 jit_solution(7182615155140139791)
XLA Ops:
  0.6 86.8 %step.1 = (f32[30720,128]{1,0:T(8,128)S(1)}, f32[32,30000]{1,0:T(8,128)S(1)}, f32[32,30000]{1,0:T(8,128)S(1)}, f32[8,32,128]{2,1,0:T(8,128)S(1)}, f32[1,1]{1,0:T(1,128)}) custom-call(bf16[32,128]{1,0:T(8,128)(2,1)} %z1.1, bf16[32,128]{1,0:T(8,128)(2,1)} %z2.1, bf16[6,32,128]{2,1,0:T(8,128)(2,1)} %zs.1, s32[1,32]{1,0:T(1,128)} %bitcast.2, ...), custom_call_target="tpu_custom_call" | custom-call | tf_op jit(solution)/shard_map/step/pallas_call | solution.py:453
  87.4 8.8 %emit.1 = (f32[32,30000]{1,0:T(8,128)}, f32[32,30000]{1,0:T(8,128)}, f32[1,1]{1,0:T(1,128)}, f32[32,128]{1,0:T(8,128)}, f32[32,128]{1,0:T(8,128)}, /*index=5*/f32[6,32,128]{2,1,0:T(8,128)}, f32[30000,128]{1,0:T(8,128)}) custom-call(f32[30720,128]{1,0:T(8,128)S(1)} %get-tuple-element.19.dc, f32[32,30000]{1,0:T(8,128)S(1)} %get-tuple-element.20.q1, ...), custom_call_target="tpu_custom_call" | custom-call | tf_op jit(solution)/shard_map/emit/pallas_call | solution.py:468

commit v4 on v3

--- a/solution.py
+++ b/solution.py
@@ -24,11 +24,11 @@
 LOGICAL = pl.DeviceIdType.LOGICAL
 VM = 36 * 1024 * 1024
 RB = 512
-NROW = 15
-RPI = KPAD // RB // NROW
-LAG2, LAG3 = 3, 7
-NIT = 2 * NCH + LAG3
 STEPS = 2 * NCH
+RPI = KPAD // RB // STEPS
+RW = RPI * RB
+QT = KP - RW * (STEPS - 1)
+LAG2, LAG3 = 2, 4
 
 
 def dot_nt(a, b):
@@ -64,8 +64,8 @@
     pltpu.make_async_copy(ref, ref, sem).wait()
 
 
-def kernel(z1, z2, zs, mask, protos, dc, q1, q2, dz, loss,
-           ca, ex, slots, lslots, wall, zall, arow, brow, gt, zl, cols, acc,
+def kernel(z1, z2, zs, mask, protos, dc, qs, qt, dz, loss,
+           ca, ex, slots, lslots, wall, zall, arow, brow, gt, xsc, gr, zl, cols, acc,
            csem, zsend, zlrecv, zs1recv, zs2send, zs2recv, arsend, arrecv, lsend, lrecv, wsend, wrecv,
            ssem, r2, r3, rs):
     me = lax.axis_index("data")
@@ -270,23 +270,26 @@
 
         def nblk(nb):
             ln = pl.ds(nb * 256, 256)
-            s = [dot_nt(c, zall[v, ln]) for v in range(VIEWS)]
-            av = [arow[v:v + 1, ln] for v in range(VIEWS)]
-            bv = [brow[v:v + 1, ln] for v in range(2)]
+            s0 = dot_nt(c, zall[0, ln])
+            s1 = dot_nt(c, zall[1, ln])
             for q in range(CB // 64):
                 sl = slice(64 * q, 64 * (q + 1))
                 w0 = jnp.concatenate([wc[0][sl], wc[0][sl]], axis=1)
                 w1 = jnp.concatenate([wc[1][sl], wc[1][sl]], axis=1)
-                p0 = jnp.exp2(s[0][sl] * SCALE)
-                p1 = jnp.exp2(s[1][sl] * SCALE)
-                x0 = (p0 * p0) * bv[0] * w0
-                x1 = (p1 * p1) * bv[1] * w1
-                xs = x0 + x1
-                gs = [p0 * av[0] - x1, p1 * av[1] - x0]
-                for v in range(2, VIEWS):
-                    gs.append(jnp.exp2(s[v][sl] * SCALE) * av[v] - xs)
-                for v in range(VIEWS):
-                    gt[nb, pl.ds(64 * q, 64), pl.ds(v * 256, 256)] = gs[v].astype(jnp.bfloat16)
+                p0 = jnp.exp2(s0[sl] * SCALE)
+                p1 = jnp.exp2(s1[sl] * SCALE)
+                x0 = (p0 * p0) * brow[0:1, ln] * w0
+                x1 = (p1 * p1) * brow[1:2, ln] * w1
+                xsc[nb, pl.ds(64 * q, 64)] = x0 + x1
+                gt[nb, pl.ds(64 * q, 64), pl.ds(0, 256)] = (p0 * arow[0:1, ln] - x1).astype(jnp.bfloat16)
+                gt[nb, pl.ds(64 * q, 64), pl.ds(256, 256)] = (p1 * arow[1:2, ln] - x0).astype(jnp.bfloat16)
+            for v in range(2, VIEWS):
+                s = dot_nt(c, zall[v, ln])
+                av = arow[v:v + 1, ln]
+                for q in range(CB // 64):
+                    sl = pl.ds(64 * q, 64)
+                    g = jnp.exp2(s[64 * q:64 * (q + 1)] * SCALE) * av - xsc[nb, sl]
+                    gt[nb, sl, pl.ds(v * 256, 256)] = g.astype(jnp.bfloat16)
             zz = jnp.concatenate([zall[v, ln] for v in range(VIEWS)], axis=0)
             return dot_nn(gt[nb], zz)
 
@@ -298,7 +301,6 @@
     def rows_part(i):
         ac = cols[0, mine]
         bc = cols[1, mine]
-        outs = []
         for h in range(RPI):
             jb = i * RPI + h
             c = ca[pl.ds(pl.multiple_of(jb * RB, RB), RB)]
@@ -315,40 +317,26 @@
             p1 = jnp.exp2(sv[1])
             o0 = (p0 * p0) * bc[:, 0:1] * wr[0]
             o1 = (p1 * p1) * bc[:, 1:2] * wr[1]
-
-            outs.append((o0, o1))
+            col = pl.ds(h * RB, RB)
+            qs[i, 0, :, col] = o0
+            qs[i, 1, :, col] = o1
             x0 = o0 * gsc
             x1 = o1 * gsc
             xs = x0 + x1
-            gs = [p0 * ac[:, 0:1] - x1, p1 * ac[:, 1:2] - x0]
+            gr[pl.ds(0, ROWS), col] = (p0 * ac[:, 0:1] - x1).astype(jnp.bfloat16)
+            gr[pl.ds(ROWS, ROWS), col] = (p1 * ac[:, 1:2] - x0).astype(jnp.bfloat16)
             ssum = sv[2]
             for v in range(3, VIEWS):
                 ssum = ssum + sv[v]
             for v in range(2, VIEWS):
-                gs.append(jnp.exp2(sv[v]) * ac[:, v:v + 1] - xs)
-            g = jnp.concatenate([x.astype(jnp.bfloat16) for x in gs], axis=0)
-            acc[pl.ds(0, VIEWS * ROWS)] += dot_nn(g, c)
+                gr[pl.ds(v * ROWS, ROWS), col] = (jnp.exp2(sv[v]) * ac[:, v:v + 1] - xs).astype(jnp.bfloat16)
             ls = x1 * sv[0] + x0 * sv[1] + xs * ssum
             part = ls[:, 0:128]
             for q in range(1, RB // 128):
                 part = part + ls[:, 128 * q:128 * (q + 1)]
             acc[pl.ds(VIEWS * ROWS, ROWS)] += part
-
-        @pl.when(i < NROW - 1)
-        def _():
-            for h in range(RPI):
-                ln = pl.ds(pl.multiple_of((i * RPI + h) * RB, RB), RB)
-                q1[:, ln] = outs[h][0]
-                q2[:, ln] = outs[h][1]
-
-        @pl.when(i == NROW - 1)
-        def _():
-            for h in range(RPI):
-                lo = ((NROW - 1) * RPI + h) * RB
-                n = min(RB, KP - lo)
-                if n > 0:
-                    q1[:, pl.ds(lo, n)] = outs[h][0][:, :n]
-                    q2[:, pl.ds(lo, n)] = outs[h][1][:, :n]
+        cs = ca[pl.ds(pl.multiple_of(i * RW, RW), RW)]
+        acc[pl.ds(0, VIEWS * ROWS)] += dot_nn(gr[...], cs)
 
     def own(it):
         for a in range(3):
@@ -374,32 +362,20 @@
                 push(owner_of(holder, d0, it), it, a, sib, rs)
 
     def main(it, carry):
-        @pl.when(it < STEPS)
-        def _():
-            with jax.named_scope("chunk"):
-                chunk(it)
-            own(it)
-
         @pl.when(it == 0)
         def _():
             with jax.named_scope("wait_w"):
                 drain(wall.at[pl.ds(0, NDEV - 1)], wrecv)
 
-        @pl.when(jnp.logical_and(it >= LAG2, it < LAG2 + STEPS))
+        with jax.named_scope("compute"):
+            chunk(it)
+            rows_part(it)
+        own(it)
+
+        @pl.when(it >= LAG2)
         def _():
             with jax.named_scope("serve2"):
                 serve2(it - LAG2)
-
-        @pl.when(it < NROW)
-        def _():
-            with jax.named_scope("rows"):
-                rows_part(it)
-
-        @pl.when(it == NROW)
-        def _():
-            total = jnp.sum(jnp.sum(acc[pl.ds(VIEWS * ROWS, ROWS)], axis=1, keepdims=True), axis=0, keepdims=True)
-            slots[4, me] = jnp.broadcast_to(total, (8, 128))
-            ar_send(4)
 
         @pl.when(it >= LAG3)
         def _():
@@ -408,8 +384,24 @@
 
         return carry
 
-    lax.fori_loop(0, NIT, main, 0)
-
+    lax.fori_loop(0, STEPS, main, 0)
+    for v in range(2):
+        qt[v] = qs[STEPS - 1, v, :, pl.ds(0, QT)]
+    total = jnp.sum(jnp.sum(acc[pl.ds(VIEWS * ROWS, ROWS)], axis=1, keepdims=True), axis=0, keepdims=True)
+    slots[4, me] = jnp.broadcast_to(total, (8, 128))
+    ar_send(4)
+
+    def rest(it, carry):
+        @pl.when(it < STEPS + LAG2)
+        def _():
+            with jax.named_scope("serve2"):
+                serve2(it - LAG2)
+
+        with jax.named_scope("serve3"):
+            serve3(it - LAG3)
+        return carry
+
+    lax.fori_loop(STEPS, STEPS + LAG3, rest, 0)
     dz[...] = acc[pl.ds(0, VIEWS * ROWS)].reshape(VIEWS, ROWS, D)
     with jax.named_scope("loss"):
         tot = ar_total(4)
@@ -433,9 +425,17 @@
     drain(wall.at[pl.ds(0, NDEV - 1)], wsend)
 
 
-def emit_kernel(dc, q1, q2, dz, loss, o_q1, o_q2, o_loss, o_z1, o_z2, o_zs, o_dc, sem):
-    pairs = [(dc.at[pl.ds(0, KP)], o_dc), (q1, o_q1), (q2, o_q2), (loss, o_loss),
-             (dz.at[0], o_z1), (dz.at[1], o_z2), (dz.at[pl.ds(2, 6)], o_zs)]
+def emit_kernel(dc, qs, qt, dz, loss, o_q1, o_q2, o_loss, o_z1, o_z2, o_zs, o_dc, sem):
+    pairs = []
+    for i in range(STEPS):
+        for v, o in enumerate((o_q1, o_q2)):
+            if i < STEPS - 1:
+                pairs.append((qs.at[i, v], o.at[:, pl.ds(i * RW, RW)]))
+            else:
+                pairs.append((qt.at[v], o.at[:, pl.ds(i * RW, QT)]))
+        rows = pl.ds(i * RW, RW if i < STEPS - 1 else QT)
+        pairs.append((dc.at[rows], o_dc.at[rows]))
+    pairs += [(loss, o_loss), (dz.at[0], o_z1), (dz.at[1], o_z2), (dz.at[pl.ds(2, 6)], o_zs)]
     copies = [pltpu.make_async_copy(a, b, sem.at[i]) for i, (a, b) in enumerate(pairs)]
     for c in copies:
         c.start()
@@ -450,15 +450,16 @@
     anym = pl.BlockSpec(memory_space=pl.ANY)
     dma = pltpu.SemaphoreType.DMA
     vm = pltpu.VMEM
-    dc, q1, q2, dz, loss = pl.pallas_call(
+    dc, qs, qt, dz, loss = pl.pallas_call(
         kernel,
-        out_shape=[vm((KPAD, D), f32), vm((ROWS, KP), f32), vm((ROWS, KP), f32),
+        out_shape=[vm((KPAD, D), f32), vm((STEPS, 2, ROWS, RW), f32), vm((2, ROWS, QT), f32),
                    vm((VIEWS, ROWS, D), f32), vm((1, 1), f32)],
         in_specs=[vmem] * 4 + [anym],
         out_specs=[vmem] * 5,
         scratch_shapes=[vm((KPAD, D), bf16), vm((2, SH, NS), f32), vm((5, NDEV, 8, 128), f32), vm((NDEV, 32, 128), f32),
                         vm((NDEV, 2, SH), f32), vm((VIEWS, NS, D), bf16), vm((8, NS), f32), vm((8, NS), f32),
-                        vm((2, CB, VIEWS * 256), bf16), vm((VIEWS * ROWS, D), bf16), vm((2, 128, 8), f32),
+                        vm((2, CB, VIEWS * 256), bf16), vm((2, CB, 256), f32),
+                        vm((VIEWS * ROWS, RW), bf16), vm((VIEWS * ROWS, D), bf16), vm((2, 128, 8), f32),
                         vm((VIEWS * ROWS + ROWS, D), f32),
                         dma, dma((2,)), dma, dma, dma, dma, dma((5,)), dma((5,)), dma, dma, dma, dma,
                         dma((STEPS, 3)), dma((STEPS, 3)), dma((STEPS, 3)), dma((STEPS, 3))],
@@ -473,10 +474,10 @@
                    jax.ShapeDtypeStruct((KP, D), f32)],
         in_specs=[vmem] * 5,
         out_specs=[anym] * 7,
-        scratch_shapes=[dma((7,))],
+        scratch_shapes=[dma((3 * STEPS + 4,))],
         compiler_params=pltpu.CompilerParams(vmem_limit_bytes=1024 * 1024),
         name="emit",
-    )(dc, q1, q2, dz, loss)
+    )(dc, qs, qt, dz, loss)
     return q1, q2, loss.reshape(()), dz1, dz2, dzs, dc
 
 

time: 96.4 us -> 92.5 us (0.960)
  Pallas kernels: 95.6 us -> 91.7 us
    pallas_call x1, Pallas kernels: 86.8 us -> 83.1 us  [local_step(): pl.pallas_call(kernel, out_shape=[vm((KPAD, D), f32), vm((STEPS, 2, ROWS,...]
where the time goes in v4:
time: 92.5 us; the launch traced here: 92.4 us
  Pallas kernels  91.7 us (99%)
    pallas_call x1, Pallas kernels, local_step(): pl.pallas_call(kernel, out_shape=[vm((KPAD, D), f32), vm((STEPS, 2, ROWS,...  83.1 us
    pallas_call x1, Pallas kernels, local_step(): pl.pallas_call(emit_kernel, out_shape=[jax.ShapeDtypeStruct((ROWS, KP), f...  8.66 us

profile of v4, /device:TPU:0, one launch (start us, length us, event | category | flops | bytes accessed | tf_op | source)
XLA Modules:
  0.0 92.4 jit_solution(10850487072767564158)
XLA Ops:
  0.6 83.1 %step.1 = (f32[30720,128]{1,0:T(8,128)S(1)}, f32[10,2,32,3072]{3,2,1,0:T(8,128)S(1)}, f32[2,32,2352]{2,1,0:T(8,128)S(1)}, f32[8,32,128]{2,1,0:T(8,128)S(1)}, f32[1,1]{1,0:T(1,128)}) custom-call(bf16[32,128]{1,0:T(8,128)(2,1)} %z1.1, bf16[32,128]{1,0:T(8,128)(2,1)} %z2.1, bf16[6,32,128]{2,1,0:T(8,128)(2,1)} %zs.1, s32[1,32]{1,0:T(1,128)} %bitcast.2, ...), custom_call_target="tpu_custom_call" | custom-call | tf_op jit(solution)/shard_map/step/pallas_call | solution.py:453
  83.7 8.7 %emit.1 = (f32[32,30000]{1,0:T(8,128)}, f32[32,30000]{1,0:T(8,128)}, f32[1,1]{1,0:T(1,128)}, f32[32,128]{1,0:T(8,128)}, f32[32,128]{1,0:T(8,128)}, /*index=5*/f32[6,32,128]{2,1,0:T(8,128)}, f32[30000,128]{1,0:T(8,128)}) custom-call(f32[30720,128]{1,0:T(8,128)S(1)} %get-tuple-element.19.dc, f32[10,2,32,3072]{3,2,1,0:T(8,128)S(1)} %get-tuple-element.20.qs, ...), custom_call_target="tpu_custom_call" | custom-call | tf_op jit(solution)/shard_map/emit/pallas_call | solution.py:469

commit v5 on v4

--- a/solution.py
+++ b/solution.py
@@ -24,11 +24,14 @@
 LOGICAL = pl.DeviceIdType.LOGICAL
 VM = 36 * 1024 * 1024
 RB = 512
-STEPS = 2 * NCH
-RPI = KPAD // RB // STEPS
+NQ = 1
+N2 = 2 * (NCH - NQ)
+STEPS = N2 + 4 * NQ
+PARTS = 15
+RPI = KPAD // RB // PARTS
 RW = RPI * RB
-QT = KP - RW * (STEPS - 1)
-LAG2, LAG3 = 2, 4
+QT = KP - RW * (PARTS - 1)
+LAG2, LAG3 = 3, 7
 
 
 def dot_nt(a, b):
@@ -65,7 +68,7 @@
 
 
 def kernel(z1, z2, zs, mask, protos, dc, qs, qt, dz, loss,
-           ca, ex, slots, lslots, wall, zall, arow, brow, gt, xsc, gr, zl, cols, acc,
+           ca, ex, mrows, slots, lslots, wall, zall, arow, brow, gt, xsc, gr, zt, px, zl, cols, acc,
            csem, zsend, zlrecv, zs1recv, zs2send, zs2recv, arsend, arrecv, lsend, lrecv, wsend, wrecv,
            ssem, r2, r3, rs):
     me = lax.axis_index("data")
@@ -74,9 +77,8 @@
     ca[pl.ds(KP, KPAD - KP), :] = jnp.zeros((KPAD - KP, D), jnp.bfloat16)
     dims = (flip(me, 2), flip(me, 4), flip(me, 8))
     sib = flip(me, 1)
-    here = lax.broadcasted_iota(jnp.int32, (8, 128), 0) == me // 4
     mpad = jnp.concatenate([mask[...].astype(jnp.float32), jnp.zeros((1, 128 - ROWS), jnp.float32)], axis=1)
-    slots[0, me] = jnp.where(here, pltpu.roll(jnp.broadcast_to(mpad, (8, 128)), ROWS * lax.rem(me, 4), 1), 0.0)
+    mrows[me] = pltpu.roll(jnp.broadcast_to(mpad, (8, 128)), ROWS * lax.rem(me, 4), 1)[0:1]
     with jax.named_scope("barrier"):
         full_barrier(me)
     myrows = pl.ds(pl.multiple_of(me * ROWS, ROWS), ROWS)
@@ -96,22 +98,26 @@
         to = lax.rem(me + d, NDEV)
         send(z1, zall.at[0, myrows], zsend.at[0], zlrecv, to)
         send(z2, zall.at[1, myrows], zsend.at[0], zlrecv, to)
-    ar_send(0)
+    for d in range(1, NDEV):
+        send(mrows.at[me], mrows.at[me], arsend.at[0], arrecv.at[0], lax.rem(me + d, NDEV))
     for d in range(1, NDEV // 2):
         send(zs, zall.at[pl.ds(2, 6), myrows], zsend.at[1], zs1recv, lax.rem(me + 2 * d, NDEV))
     zall[0, myrows] = z1[...]
     zall[1, myrows] = z2[...]
     zall[pl.ds(2, 6), myrows] = zs[...]
     send(zs, zall.at[pl.ds(2, 6), myrows], zs2send, zs2recv, sib)
-    zl[pl.ds(0, ROWS)] = z1[...]
-    zl[pl.ds(ROWS, ROWS)] = z2[...]
-    zl[pl.ds(2 * ROWS, 6 * ROWS)] = zs[...].reshape(6 * ROWS, D)
+    zl[pl.ds(0, ROWS), pl.ds(0, D)] = z1[...]
+    zl[pl.ds(ROWS, ROWS), pl.ds(0, D)] = z2[...]
+    zl[pl.ds(2 * ROWS, 6 * ROWS), pl.ds(0, D)] = zs[...].reshape(6 * ROWS, D)
+    zl[pl.ds(0, 2 * ROWS), pl.ds(D, 128)] = jnp.zeros((2 * ROWS, 128), jnp.bfloat16)
     acc[...] = jnp.zeros_like(acc)
     cc.wait()
     with jax.named_scope("mask"):
-        mask8 = ar_total(0)
-    live = jnp.sum(jnp.sum(mask8, axis=1, keepdims=True), axis=0, keepdims=True)
-    mrow = jnp.concatenate([mask8[j:j + 1] for j in range(4)], axis=1)
+        drain(mrows.at[pl.ds(0, NDEV - 1)], arrecv.at[0])
+        mask8 = [mrows[4 * j] + mrows[4 * j + 1] + mrows[4 * j + 2] + mrows[4 * j + 3] for j in range(4)]
+    mask4 = jnp.concatenate(mask8, axis=0)
+    mrow = jnp.concatenate(mask8, axis=1)
+    live = jnp.sum(jnp.sum(mask4, axis=1, keepdims=True), axis=0, keepdims=True)
     with jax.named_scope("zlarge"):
         drain(zall.at[pl.ds(0, 2), pl.ds(0, NS - ROWS)], zlrecv)
 
@@ -225,18 +231,33 @@
         tot = lslots[0]
         for i in range(1, NDEV):
             tot = tot + lslots[i]
-        inv = 1.0 / tot
-        for v in range(VIEWS):
+        logs = jnp.log(tot)
+        inv = 1.0 / tot[0:8]
+        for v in range(2):
             for j in range(4):
-                coef = 1.0 if v < 2 else 2.0
-                arow[v:v + 1, 128 * j:128 * (j + 1)] = (coef * gsc) * (mask8[j:j + 1] * inv[4 * v + j:4 * v + j + 1])
-        weight = jnp.concatenate([mask8[0:4]] * 2 + [2.0 * mask8[0:4]] * 6, axis=0)
-        lsum = jnp.sum(jnp.sum(weight * jnp.log(tot), axis=1, keepdims=True), axis=0, keepdims=True)
+                arow[v:v + 1, 128 * j:128 * (j + 1)] = gsc * (mask8[j] * inv[4 * v + j:4 * v + j + 1])
+        lg2 = jnp.log(2.0 * gsc)
+        lsum = jnp.sum(jnp.sum(jnp.concatenate([mask4] * 2, axis=0) * logs[0:8], axis=1, keepdims=True), axis=0, keepdims=True)
+        lsum = lsum + (12.0 * live) * lg2
+        rest_ = jnp.where(jnp.concatenate([mask4] * 8, axis=0) > 0, TAU * (lg2 - logs), -100.0)
+        for k in range(3):
+            piece_ = rest_.astype(jnp.bfloat16).astype(jnp.float32)
+            px[k] = piece_
+            rest_ = rest_ - piece_
+        for j in range(4):
+            block = jnp.concatenate([px[k, pl.ds(8 + j, 6, 4)] for k in range(3)] + [jnp.zeros((110, 128), jnp.float32)], axis=0)
+            zt[pl.ds(128 * j, 128)] = block.T.astype(jnp.bfloat16)
+        lane = lax.broadcasted_iota(jnp.int32, (ROWS, 128), 1)
+        own_rows = zt[myrows].astype(jnp.float32)
+        for v in range(2, VIEWS):
+            pick = jnp.where(jnp.logical_and(lax.rem(lane, 6) == v - 2, lane < 18), own_rows, 0.0)
+            zl[pl.ds(v * ROWS, ROWS), pl.ds(D, 128)] = pick.astype(jnp.bfloat16)
     with jax.named_scope("ar3"):
         us = scale_rows(ar_total(3))
     for v in range(2):
         brow[v:v + 1] = live * us[v]
     brow[2:8] = jnp.zeros((6, NS), jnp.float32)
+    arow[2:8] = jnp.zeros((6, NS), jnp.float32)
     tile = pl.ds(pl.multiple_of((me // 4) * 128, 128), 128)
     cols[0] = arow[:, tile].T
     cols[1] = brow[:, tile].T
@@ -245,19 +266,27 @@
     def piece_row(owner, t, a):
         return pl.multiple_of(owner * SH + t * CB + a * 128, 128)
 
+    def parts_of(it):
+        quad = (it + 8 - N2) // 8
+        t = (1 - quad) * (it // 2) + quad * (NCH - NQ + (it - N2) // 4)
+        par = (1 - quad) * lax.rem(it, 2) + quad * lax.rem(it + 4 - N2 % 4, 4)
+        return t, par
+
     def push(owner, it, a, to, rsem):
-        ref = dc.at[pl.ds(piece_row(owner, it // 2, a), 128)]
+        ref = dc.at[pl.ds(piece_row(owner, parts_of(it)[0], a), 128)]
         send(ref, ref, ssem.at[it, a], rsem.at[it, a], to)
 
     def order(a):
         return dims[a], dims[(a + 1) % 3], dims[(a + 2) % 3]
 
-    def owner_of(holder, d0, it):
-        return holder + lax.rem(it, 2) * (d0 - me)
+    def owner_of(holder, a, it):
+        d0, d1, _ = order(a)
+        par = parts_of(it)[1]
+        return holder + lax.rem(par, 2) * (d0 - me) + (par // 2) * (d1 - me)
 
     def chunk(it):
-        t = it // 2
-        owners = [owner_of(me, dims[a], it) for a in range(3)]
+        t = parts_of(it)[0]
+        owners = [owner_of(me, a, it) for a in range(3)]
         c = jnp.concatenate([ca[pl.ds(piece_row(owners[a], t, a), 128)] for a in range(3)], axis=0)
         wc = []
         for v in range(2):
@@ -267,44 +296,60 @@
                 row = wall[owners[a], pl.ds(v, 1), pl.ds(off, 128)] * gsc
                 parts.append(jnp.broadcast_to(row, (128, 128)).T)
             wc.append(jnp.concatenate(parts, axis=0))
-
-        def nblk(nb):
-            ln = pl.ds(nb * 256, 256)
-            s0 = dot_nt(c, zall[0, ln])
-            s1 = dot_nt(c, zall[1, ln])
-            for q in range(CB // 64):
-                sl = slice(64 * q, 64 * (q + 1))
-                w0 = jnp.concatenate([wc[0][sl], wc[0][sl]], axis=1)
-                w1 = jnp.concatenate([wc[1][sl], wc[1][sl]], axis=1)
-                p0 = jnp.exp2(s0[sl] * SCALE)
-                p1 = jnp.exp2(s1[sl] * SCALE)
-                x0 = (p0 * p0) * brow[0:1, ln] * w0
-                x1 = (p1 * p1) * brow[1:2, ln] * w1
-                xsc[nb, pl.ds(64 * q, 64)] = x0 + x1
-                gt[nb, pl.ds(64 * q, 64), pl.ds(0, 256)] = (p0 * arow[0:1, ln] - x1).astype(jnp.bfloat16)
-                gt[nb, pl.ds(64 * q, 64), pl.ds(256, 256)] = (p1 * arow[1:2, ln] - x0).astype(jnp.bfloat16)
-            for v in range(2, VIEWS):
-                s = dot_nt(c, zall[v, ln])
-                av = arow[v:v + 1, ln]
-                for q in range(CB // 64):
-                    sl = pl.ds(64 * q, 64)
-                    g = jnp.exp2(s[64 * q:64 * (q + 1)] * SCALE) * av - xsc[nb, sl]
-                    gt[nb, sl, pl.ds(v * 256, 256)] = g.astype(jnp.bfloat16)
-            zz = jnp.concatenate([zall[v, ln] for v in range(VIEWS)], axis=0)
-            return dot_nn(gt[nb], zz)
-
-        res = nblk(0)
-        res = res + nblk(1)
+        QR = 32
+        lanes = lax.broadcasted_iota(jnp.int32, (CB, 128), 1)
+        HALF = CB // 2
+        LW = 256
+
+        def put_g(v, q, l, g):
+            gt[v // 4, pl.ds(QR * q, QR), pl.ds((v % 4) * NS + LW * l, LW)] = g.astype(jnp.bfloat16)
+
+        def dc_part(h):
+            zz = zall[pl.ds(4 * h, 4)].reshape(4 * NS, D)
+            return [dot_nn(gt[h, pl.ds(HALF * m, HALF)], zz) for m in range(2)]
+
+        def rows_of(ref, v, l):
+            return ref[v:v + 1, LW * l:LW * (l + 1)]
+
+        s0 = dot_nt(c, zall[0])
+        s1 = dot_nt(c, zall[1])
+        for l in range(NS // LW):
+            b0, b1, a0, a1 = rows_of(brow, 0, l), rows_of(brow, 1, l), rows_of(arow, 0, l), rows_of(arow, 1, l)
+            ln = slice(LW * l, LW * (l + 1))
+            for q in range(CB // QR):
+                sl = slice(QR * q, QR * (q + 1))
+                p0 = jnp.exp2(s0[sl, ln] * SCALE)
+                p1 = jnp.exp2(s1[sl, ln] * SCALE)
+                x0 = (p0 * p0) * b0 * jnp.concatenate([wc[0][sl]] * 2, axis=1)
+                x1 = (p1 * p1) * b1 * jnp.concatenate([wc[1][sl]] * 2, axis=1)
+                xsc[pl.ds(QR * q, QR), pl.ds(LW * l, LW)] = x0 + x1
+                put_g(0, q, l, p0 * a0 - x1)
+                put_g(1, q, l, p1 * a1 - x0)
+        res = None
+        for v in range(2, VIEWS):
+            sel = jnp.where(jnp.logical_and(lax.rem(lanes, 6) == v - 2, lanes < 18), 1.0, 0.0).astype(jnp.bfloat16)
+            s = dot_nt(jnp.concatenate([c, sel], axis=1), jnp.concatenate([zall[v], zt[...]], axis=1))
+            for l in range(NS // LW):
+                ln = slice(LW * l, LW * (l + 1))
+                for q in range(CB // QR):
+                    sl = slice(QR * q, QR * (q + 1))
+                    put_g(v, q, l, jnp.exp2(s[sl, ln] * SCALE) - xsc[pl.ds(QR * q, QR), pl.ds(LW * l, LW)])
+            if v == 3:
+                res = dc_part(0)
+        more = dc_part(1)
+        out = jnp.concatenate([res[0] + more[0], res[1] + more[1]], axis=0)
         for a in range(3):
-            dc[pl.ds(piece_row(owners[a], t, a), 128)] = res[128 * a:128 * (a + 1)]
+            dc[pl.ds(piece_row(owners[a], t, a), 128)] = out[128 * a:128 * (a + 1)]
 
     def rows_part(i):
         ac = cols[0, mine]
         bc = cols[1, mine]
+        lanes = lax.broadcasted_iota(jnp.int32, (RB, 128), 1)
+        ones = jnp.where(lanes < 18, 1.0, 0.0).astype(jnp.bfloat16)
         for h in range(RPI):
             jb = i * RPI + h
             c = ca[pl.ds(pl.multiple_of(jb * RB, RB), RB)]
-            s = dot_nt(zl[...], c) * SCALE
+            s = dot_nt(zl[...], jnp.concatenate([c, ones], axis=1)) * SCALE
             wr = []
             for v in range(2):
                 parts = []
@@ -329,7 +374,7 @@
             for v in range(3, VIEWS):
                 ssum = ssum + sv[v]
             for v in range(2, VIEWS):
-                gr[pl.ds(v * ROWS, ROWS), col] = (jnp.exp2(sv[v]) * ac[:, v:v + 1] - xs).astype(jnp.bfloat16)
+                gr[pl.ds(v * ROWS, ROWS), col] = (jnp.exp2(sv[v]) - xs).astype(jnp.bfloat16)
             ls = x1 * sv[0] + x0 * sv[1] + xs * ssum
             part = ls[:, 0:128]
             for q in range(1, RB // 128):
@@ -340,39 +385,56 @@
 
     def own(it):
         for a in range(3):
-            d0, d1, d2 = order(a)
-            o = owner_of(me, d0, it)
-            push(o, it, a, d1, r2)
-            push(o, it, a, d2, r3)
+            o = owner_of(me, a, it)
+            push(o, it, a, order(a)[2], r3)
             push(o, it, a, sib, rs)
+
+    def own1(it):
+        for a in range(3):
+            push(owner_of(me, a, it), it, a, order(a)[1], r2)
 
     def serve2(it):
         for a in range(3):
             d0, d1, d2 = order(a)
             drain(dc.at[pl.ds(0, 128)], r2.at[it, a])
-            o = owner_of(d1, d0, it)
+            o = owner_of(d1, a, it)
             push(o, it, a, d2, r3)
             push(o, it, a, sib, rs)
 
     def serve3(it):
-        for a in range(3):
-            d0, d1, d2 = order(a)
-            drain(dc.at[pl.ds(0, 256)], r3.at[it, a])
-            for holder in (d2, d2 + d1 - me):
-                push(owner_of(holder, d0, it), it, a, sib, rs)
+        @pl.when(it < N2)
+        def _():
+            for a in range(3):
+                d0, d1, d2 = order(a)
+                drain(dc.at[pl.ds(0, 256)], r3.at[it, a])
+                for holder in (d2, d2 + d1 - me):
+                    push(owner_of(holder, a, it), it, a, sib, rs)
+
+        @pl.when(it >= N2)
+        def _():
+            for a in range(3):
+                drain(dc.at[pl.ds(0, 128)], r3.at[it, a])
+                push(owner_of(order(a)[2], a, it), it, a, sib, rs)
+
+    with jax.named_scope("chunk0"):
+        chunk(0)
+    own1(0)
+    own(0)
+    with jax.named_scope("wait_w"):
+        drain(wall.at[pl.ds(0, NDEV - 1)], wrecv)
 
     def main(it, carry):
-        @pl.when(it == 0)
-        def _():
-            with jax.named_scope("wait_w"):
-                drain(wall.at[pl.ds(0, NDEV - 1)], wrecv)
-
         with jax.named_scope("compute"):
             chunk(it)
-            rows_part(it)
+            rows_part(it - 1)
+
+        @pl.when(it < N2)
+        def _():
+            own1(it)
+
         own(it)
 
-        @pl.when(it >= LAG2)
+        @pl.when(jnp.logical_and(it >= LAG2, it < LAG2 + N2))
         def _():
             with jax.named_scope("serve2"):
                 serve2(it - LAG2)
@@ -384,24 +446,26 @@
 
         return carry
 
-    lax.fori_loop(0, STEPS, main, 0)
+    lax.fori_loop(1, STEPS, main, 0)
+
+    def rest(i, carry):
+        with jax.named_scope("rows"):
+            rows_part(i)
+        return carry
+
+    lax.fori_loop(STEPS - 1, PARTS, rest, 0)
     for v in range(2):
-        qt[v] = qs[STEPS - 1, v, :, pl.ds(0, QT)]
+        qt[v] = qs[PARTS - 1, v, :, pl.ds(0, QT)]
     total = jnp.sum(jnp.sum(acc[pl.ds(VIEWS * ROWS, ROWS)], axis=1, keepdims=True), axis=0, keepdims=True)
     slots[4, me] = jnp.broadcast_to(total, (8, 128))
     ar_send(4)
 
-    def rest(it, carry):
-        @pl.when(it < STEPS + LAG2)
-        def _():
-            with jax.named_scope("serve2"):
-                serve2(it - LAG2)
-
+    def last(it, carry):
         with jax.named_scope("serve3"):
-            serve3(it - LAG3)
+            serve3(it)
         return carry
 
-    lax.fori_loop(STEPS, STEPS + LAG3, rest, 0)
+    lax.fori_loop(STEPS - LAG3, STEPS, last, 0)
     dz[...] = acc[pl.ds(0, VIEWS * ROWS)].reshape(VIEWS, ROWS, D)
     with jax.named_scope("loss"):
         tot = ar_total(4)
@@ -409,9 +473,17 @@
     loss[...] = -cross / (live * PAIRS)
 
     def finish(it, carry):
-        for a in range(3):
-            drain(dc.at[pl.ds(0, 4 * 128)], rs.at[it, a])
-            drain(dc.at[pl.ds(0, 7 * 128)], ssem.at[it, a])
+        @pl.when(it < N2)
+        def _():
+            for a in range(3):
+                drain(dc.at[pl.ds(0, 4 * 128)], rs.at[it, a])
+                drain(dc.at[pl.ds(0, 7 * 128)], ssem.at[it, a])
+
+        @pl.when(it >= N2)
+        def _():
+            for a in range(3):
+                drain(dc.at[pl.ds(0, 2 * 128)], rs.at[it, a])
+                drain(dc.at[pl.ds(0, 3 * 128)], ssem.at[it, a])
         return carry
 
     with jax.named_scope("finish"):
@@ -419,7 +491,8 @@
     drain(zall.at[pl.ds(0, 2), pl.ds(0, NS - ROWS)], zsend.at[0])
     drain(zall.at[pl.ds(2, 6), pl.ds(0, 7 * ROWS)], zsend.at[1])
     drain(zall.at[pl.ds(2, 6), pl.ds(0, 8 * ROWS)], zs2send)
-    for t in range(5):
+    drain(mrows.at[pl.ds(0, NDEV - 1)], arsend.at[0])
+    for t in range(1, 5):
         drain(slots.at[t, pl.ds(0, NDEV - 1)], arsend.at[t])
     drain(lslots.at[pl.ds(0, NDEV - 1)], lsend)
     drain(wall.at[pl.ds(0, NDEV - 1)], wsend)
@@ -427,13 +500,13 @@
 
 def emit_kernel(dc, qs, qt, dz, loss, o_q1, o_q2, o_loss, o_z1, o_z2, o_zs, o_dc, sem):
     pairs = []
-    for i in range(STEPS):
+    for i in range(PARTS):
         for v, o in enumerate((o_q1, o_q2)):
-            if i < STEPS - 1:
+            if i < PARTS - 1:
                 pairs.append((qs.at[i, v], o.at[:, pl.ds(i * RW, RW)]))
             else:
                 pairs.append((qt.at[v], o.at[:, pl.ds(i * RW, QT)]))
-        rows = pl.ds(i * RW, RW if i < STEPS - 1 else QT)
+        rows = pl.ds(i * RW, RW if i < PARTS - 1 else QT)
         pairs.append((dc.at[rows], o_dc.at[rows]))
     pairs += [(loss, o_loss), (dz.at[0], o_z1), (dz.at[1], o_z2), (dz.at[pl.ds(2, 6)], o_zs)]
     copies = [pltpu.make_async_copy(a, b, sem.at[i]) for i, (a, b) in enumerate(pairs)]
@@ -452,14 +525,15 @@
     vm = pltpu.VMEM
     dc, qs, qt, dz, loss = pl.pallas_call(
         kernel,
-        out_shape=[vm((KPAD, D), f32), vm((STEPS, 2, ROWS, RW), f32), vm((2, ROWS, QT), f32),
+        out_shape=[vm((KPAD, D), f32), vm((PARTS, 2, ROWS, RW), f32), vm((2, ROWS, QT), f32),
                    vm((VIEWS, ROWS, D), f32), vm((1, 1), f32)],
         in_specs=[vmem] * 4 + [anym],
         out_specs=[vmem] * 5,
-        scratch_shapes=[vm((KPAD, D), bf16), vm((2, SH, NS), f32), vm((5, NDEV, 8, 128), f32), vm((NDEV, 32, 128), f32),
+        scratch_shapes=[vm((KPAD, D), bf16), vm((2, SH, NS), f32), vm((NDEV, 1, 128), f32), vm((5, NDEV, 8, 128), f32), vm((NDEV, 32, 128), f32),
                         vm((NDEV, 2, SH), f32), vm((VIEWS, NS, D), bf16), vm((8, NS), f32), vm((8, NS), f32),
-                        vm((2, CB, VIEWS * 256), bf16), vm((2, CB, 256), f32),
-                        vm((VIEWS * ROWS, RW), bf16), vm((VIEWS * ROWS, D), bf16), vm((2, 128, 8), f32),
+                        vm((2, CB, 4 * NS), bf16), vm((CB, NS), f32),
+                        vm((VIEWS * ROWS, RW), bf16), vm((NS, 128), bf16), vm((3, 32, 128), f32), vm((VIEWS * ROWS, 2 * D), bf16),
+                        vm((2, 128, 8), f32),
                         vm((VIEWS * ROWS + ROWS, D), f32),
                         dma, dma((2,)), dma, dma, dma, dma, dma((5,)), dma((5,)), dma, dma, dma, dma,
                         dma((STEPS, 3)), dma((STEPS, 3)), dma((STEPS, 3)), dma((STEPS, 3))],
@@ -474,7 +548,7 @@
                    jax.ShapeDtypeStruct((KP, D), f32)],
         in_specs=[vmem] * 5,
         out_specs=[anym] * 7,
-        scratch_shapes=[dma((3 * STEPS + 4,))],
+        scratch_shapes=[dma((3 * PARTS + 4,))],
         compiler_params=pltpu.CompilerParams(vmem_limit_bytes=1024 * 1024),
         name="emit",
     )(dc, qs, qt, dz, loss)

time: 92.5 us -> 87.1 us (0.942)
  Pallas kernels: 91.7 us -> 86.3 us
    pallas_call x1, Pallas kernels: 83.1 us -> 77.5 us  [local_step(): pl.pallas_call(kernel, out_shape=[vm((KPAD, D), f32), vm((PARTS, 2, ROWS,...]
where the time goes in v5:
time: 87.1 us; the launch traced here: 86.9 us
  Pallas kernels  86.3 us (99%)
    pallas_call x1, Pallas kernels, local_step(): pl.pallas_call(kernel, out_shape=[vm((KPAD, D), f32), vm((PARTS, 2, ROWS,...  77.5 us
    pallas_call x1, Pallas kernels, local_step(): pl.pallas_call(emit_kernel, out_shape=[jax.ShapeDtypeStruct((ROWS, KP), f...  8.78 us

profile of v5, /device:TPU:0, one launch (start us, length us, event | category | flops | bytes accessed | tf_op | source)
XLA Modules:
  0.0 86.9 jit_solution(635853255533338054)
XLA Ops:
  0.6 77.5 %step.1 = (f32[30720,128]{1,0:T(8,128)S(1)}, f32[15,2,32,2048]{3,2,1,0:T(8,128)S(1)}, f32[2,32,1328]{2,1,0:T(8,128)S(1)}, f32[8,32,128]{2,1,0:T(8,128)S(1)}, f32[1,1]{1,0:T(1,128)}) custom-call(bf16[32,128]{1,0:T(8,128)(2,1)} %z1.1, bf16[32,128]{1,0:T(8,128)(2,1)} %z2.1, bf16[6,32,128]{2,1,0:T(8,128)(2,1)} %zs.1, s32[1,32]{1,0:T(1,128)} %bitcast.2, ...), custom_call_target="tpu_custom_call" | custom-call | tf_op jit(solution)/shard_map/step/pallas_call | solution.py:526
  78.1 8.8 %emit.1 = (f32[32,30000]{1,0:T(8,128)}, f32[32,30000]{1,0:T(8,128)}, f32[1,1]{1,0:T(1,128)}, f32[32,128]{1,0:T(8,128)}, f32[32,128]{1,0:T(8,128)}, /*index=5*/f32[6,32,128]{2,1,0:T(8,128)}, f32[30000,128]{1,0:T(8,128)}) custom-call(f32[30720,128]{1,0:T(8,128)S(1)} %get-tuple-element.19.dc, f32[15,2,32,2048]{3,2,1,0:T(8,128)S(1)} %get-tuple-element.20.qs, ...), custom_call_target="tpu_custom_call" | custom-call | tf_op jit(solution)/shard_map/emit/pallas_call | solution.py:543

commit v6 on v5

--- a/solution.py
+++ b/solution.py
@@ -32,6 +32,13 @@
 RW = RPI * RB
 QT = KP - RW * (PARTS - 1)
 LAG2, LAG3 = 3, 7
+LANE = 128
+OTHERS = NDEV - 1
+CROPS = pl.ds(2, 6)
+SMALL = range(2, VIEWS)
+PEERS = range(1, NDEV)
+PEERS_HALF = range(1, NDEV // 2)
+QR, LW = 32, 256
 
 
 def dot_nt(a, b):
@@ -52,9 +59,9 @@
 
 def full_barrier(me):
     barrier = pltpu.get_barrier_semaphore()
-    for d in range(1, NDEV):
+    for d in PEERS:
         pl.semaphore_signal(barrier, inc=1, device_id=lax.rem(me + d, NDEV), device_id_type=LOGICAL)
-    pl.semaphore_wait(barrier, NDEV - 1)
+    pl.semaphore_wait(barrier, OTHERS)
 
 
 def send(src, dst, ssem, rsem, to):
@@ -77,43 +84,43 @@
     ca[pl.ds(KP, KPAD - KP), :] = jnp.zeros((KPAD - KP, D), jnp.bfloat16)
     dims = (flip(me, 2), flip(me, 4), flip(me, 8))
     sib = flip(me, 1)
-    mpad = jnp.concatenate([mask[...].astype(jnp.float32), jnp.zeros((1, 128 - ROWS), jnp.float32)], axis=1)
-    mrows[me] = pltpu.roll(jnp.broadcast_to(mpad, (8, 128)), ROWS * lax.rem(me, 4), 1)[0:1]
+    mpad = jnp.concatenate([mask[...].astype(jnp.float32), jnp.zeros((1, LANE - ROWS), jnp.float32)], axis=1)
+    mrows[me] = pltpu.roll(jnp.broadcast_to(mpad, (8, LANE)), ROWS * lax.rem(me, 4), 1)[0:1]
     with jax.named_scope("barrier"):
         full_barrier(me)
     myrows = pl.ds(pl.multiple_of(me * ROWS, ROWS), ROWS)
 
     def ar_send(t):
-        for d in range(1, NDEV):
+        for d in PEERS:
             send(slots.at[t, me], slots.at[t, me], arsend.at[t], arrecv.at[t], lax.rem(me + d, NDEV))
 
     def ar_total(t):
-        drain(slots.at[t, pl.ds(0, NDEV - 1)], arrecv.at[t])
+        drain(slots.at[t, pl.ds(0, OTHERS)], arrecv.at[t])
         tot = slots[t, 0]
-        for i in range(1, NDEV):
+        for i in PEERS:
             tot = tot + slots[t, i]
         return tot
 
-    for d in range(1, NDEV):
+    for d in PEERS:
         to = lax.rem(me + d, NDEV)
         send(z1, zall.at[0, myrows], zsend.at[0], zlrecv, to)
         send(z2, zall.at[1, myrows], zsend.at[0], zlrecv, to)
-    for d in range(1, NDEV):
+    for d in PEERS:
         send(mrows.at[me], mrows.at[me], arsend.at[0], arrecv.at[0], lax.rem(me + d, NDEV))
-    for d in range(1, NDEV // 2):
-        send(zs, zall.at[pl.ds(2, 6), myrows], zsend.at[1], zs1recv, lax.rem(me + 2 * d, NDEV))
+    for d in PEERS_HALF:
+        send(zs, zall.at[CROPS, myrows], zsend.at[1], zs1recv, lax.rem(me + 2 * d, NDEV))
     zall[0, myrows] = z1[...]
     zall[1, myrows] = z2[...]
-    zall[pl.ds(2, 6), myrows] = zs[...]
-    send(zs, zall.at[pl.ds(2, 6), myrows], zs2send, zs2recv, sib)
+    zall[CROPS, myrows] = zs[...]
+    send(zs, zall.at[CROPS, myrows], zs2send, zs2recv, sib)
     zl[pl.ds(0, ROWS), pl.ds(0, D)] = z1[...]
     zl[pl.ds(ROWS, ROWS), pl.ds(0, D)] = z2[...]
     zl[pl.ds(2 * ROWS, 6 * ROWS), pl.ds(0, D)] = zs[...].reshape(6 * ROWS, D)
-    zl[pl.ds(0, 2 * ROWS), pl.ds(D, 128)] = jnp.zeros((2 * ROWS, 128), jnp.bfloat16)
+    zl[pl.ds(0, 2 * ROWS), pl.ds(D, LANE)] = jnp.zeros((2 * ROWS, LANE), jnp.bfloat16)
     acc[...] = jnp.zeros_like(acc)
     cc.wait()
     with jax.named_scope("mask"):
-        drain(mrows.at[pl.ds(0, NDEV - 1)], arrecv.at[0])
+        drain(mrows.at[pl.ds(0, OTHERS)], arrecv.at[0])
         mask8 = [mrows[4 * j] + mrows[4 * j + 1] + mrows[4 * j + 2] + mrows[4 * j + 3] for j in range(4)]
     mask4 = jnp.concatenate(mask8, axis=0)
     mrow = jnp.concatenate(mask8, axis=1)
@@ -122,7 +129,7 @@
         drain(zall.at[pl.ds(0, 2), pl.ds(0, NS - ROWS)], zlrecv)
 
     def shard(b):
-        return ca[pl.ds(pl.multiple_of(me * SH + b * CB, 128), CB)]
+        return ca[pl.ds(pl.multiple_of(me * SH + b * CB, LANE), CB)]
 
     def col_scale(c, b):
         k = me * SH + b * CB + lax.broadcasted_iota(jnp.int32, (CB, 1), 0)
@@ -148,7 +155,7 @@
         for v, r in enumerate((r1, r2)):
             row = jnp.sum(r, axis=0, keepdims=True)
             for j in range(4):
-                slots[t, me, pl.ds(4 * v + j, 1)] = row[:, 128 * j:128 * (j + 1)]
+                slots[t, me, pl.ds(4 * v + j, 1)] = row[:, LANE * j:LANE * (j + 1)]
 
     def scale_rows(tot):
         us = []
@@ -157,12 +164,12 @@
             us.append(mrow / (live * jnp.where(mrow > 0, r, 1.0)))
         return us
 
-    pad = jnp.where(me == NDEV - 1, float(SH - LAST), 0.0)
+    pad = jnp.where(me == OTHERS, float(SH - LAST), 0.0)
 
     def put_lse(v, ps):
         row = jnp.sum(ps, axis=0, keepdims=True) - pad
         for j in range(4):
-            lslots[me, pl.ds(4 * v + j, 1)] = row[:, 128 * j:128 * (j + 1)]
+            lslots[me, pl.ds(4 * v + j, 1)] = row[:, LANE * j:LANE * (j + 1)]
 
     with jax.named_scope("first"):
         carry = (zero8,) * 4
@@ -174,10 +181,11 @@
     put_lse(0, ps1)
     put_lse(1, ps2)
     with jax.named_scope("zsmall1"):
-        drain(zall.at[pl.ds(2, 6), pl.ds(0, 7 * ROWS)], zs1recv)
-    for d in range(1, NDEV // 2):
+        drain(zall.at[CROPS, pl.ds(0, 7 * ROWS)], zs1recv)
+    for d in PEERS_HALF:
         rows = pl.ds(pl.multiple_of(lax.rem(me + 2 * d, NDEV) * ROWS, ROWS), ROWS)
-        send(zall.at[pl.ds(2, 6), rows], zall.at[pl.ds(2, 6), rows], zs2send, zs2recv, sib)
+        send(zall.at[CROPS, rows], zall.at[CROPS, rows], zs2send, zs2recv, sib)
+
     def small(i, carry):
         v = 2 + i
         ps = zero8
@@ -187,7 +195,7 @@
         return carry
 
     with jax.named_scope("zsmall2"):
-        drain(zall.at[pl.ds(2, 6), pl.ds(0, 8 * ROWS)], zs2recv)
+        drain(zall.at[CROPS, pl.ds(0, 8 * ROWS)], zs2recv)
 
     with jax.named_scope("small"):
         lax.fori_loop(0, 3, small, 0)
@@ -203,9 +211,9 @@
                 w = col_scale(jnp.sum(e * us[v], axis=1, keepdims=True), b)
                 out.append(carry[v] + fold8(e * w))
                 if last:
-                    for q in range(CB // 128):
-                        wt = jnp.broadcast_to(w[128 * q:128 * (q + 1)], (128, 128)).T
-                        wall[me, pl.ds(v, 1), pl.ds(pl.multiple_of(b * CB + 128 * q, 128), 128)] = wt[0:1]
+                    for q in range(CB // LANE):
+                        wt = jnp.broadcast_to(w[LANE * q:LANE * (q + 1)], (LANE, LANE)).T
+                        wall[me, pl.ds(v, 1), pl.ds(pl.multiple_of(b * CB + LANE * q, LANE), LANE)] = wt[0:1]
             return tuple(out)
         return step
 
@@ -215,7 +223,7 @@
         ar_send(2)
     with jax.named_scope("small"):
         lax.fori_loop(3, 6, small, 0)
-        for d in range(1, NDEV):
+        for d in PEERS:
             send(lslots.at[me], lslots.at[me], lsend, lrecv, lax.rem(me + d, NDEV))
     with jax.named_scope("ar2"):
         us = scale_rows(ar_total(2))
@@ -223,19 +231,19 @@
         r1, rr2 = lax.fori_loop(0, NCH, again(us, True), (zero8, zero8))
         put(3, r1, rr2)
         ar_send(3)
-        for d in range(1, NDEV):
+        for d in PEERS:
             send(wall.at[me], wall.at[me], wsend, wrecv, lax.rem(me + d, NDEV))
     gsc = 1.0 / (TAU * PAIRS * live)
     with jax.named_scope("lse"):
-        drain(lslots.at[pl.ds(0, NDEV - 1)], lrecv)
+        drain(lslots.at[pl.ds(0, OTHERS)], lrecv)
         tot = lslots[0]
-        for i in range(1, NDEV):
+        for i in PEERS:
             tot = tot + lslots[i]
         logs = jnp.log(tot)
         inv = 1.0 / tot[0:8]
         for v in range(2):
             for j in range(4):
-                arow[v:v + 1, 128 * j:128 * (j + 1)] = gsc * (mask8[j] * inv[4 * v + j:4 * v + j + 1])
+                arow[v:v + 1, LANE * j:LANE * (j + 1)] = gsc * (mask8[j] * inv[4 * v + j:4 * v + j + 1])
         lg2 = jnp.log(2.0 * gsc)
         lsum = jnp.sum(jnp.sum(jnp.concatenate([mask4] * 2, axis=0) * logs[0:8], axis=1, keepdims=True), axis=0, keepdims=True)
         lsum = lsum + (12.0 * live) * lg2
@@ -245,26 +253,36 @@
             px[k] = piece_
             rest_ = rest_ - piece_
         for j in range(4):
-            block = jnp.concatenate([px[k, pl.ds(8 + j, 6, 4)] for k in range(3)] + [jnp.zeros((110, 128), jnp.float32)], axis=0)
-            zt[pl.ds(128 * j, 128)] = block.T.astype(jnp.bfloat16)
-        lane = lax.broadcasted_iota(jnp.int32, (ROWS, 128), 1)
+            block = jnp.concatenate([px[k, pl.ds(8 + j, 6, 4)] for k in range(3)] + [jnp.zeros((110, LANE), jnp.float32)], axis=0)
+            zt[pl.ds(LANE * j, LANE)] = block.T.astype(jnp.bfloat16)
+        lane = lax.broadcasted_iota(jnp.int32, (ROWS, LANE), 1)
         own_rows = zt[myrows].astype(jnp.float32)
-        for v in range(2, VIEWS):
+        for v in SMALL:
             pick = jnp.where(jnp.logical_and(lax.rem(lane, 6) == v - 2, lane < 18), own_rows, 0.0)
-            zl[pl.ds(v * ROWS, ROWS), pl.ds(D, 128)] = pick.astype(jnp.bfloat16)
+            zl[pl.ds(v * ROWS, ROWS), pl.ds(D, LANE)] = pick.astype(jnp.bfloat16)
+    def probs(c, v):
+        if v < 2:
+            return dot_nt(c, zall[v])
+        lanes = lax.broadcasted_iota(jnp.int32, (CB, LANE), 1)
+        sel = jnp.where(jnp.logical_and(lax.rem(lanes, 6) == v - 2, lanes < 18), 1.0, 0.0).astype(jnp.bfloat16)
+        return dot_nt(jnp.concatenate([c, sel], axis=1), jnp.concatenate([zall[v], zt[...]], axis=1))
+
+    with jax.named_scope("ahead"):
+        for v in range(VIEWS):
+            ex[v % 2, pl.ds(v // 2 * CB, CB)] = jnp.exp2(probs(shard(0), v) * SCALE)
     with jax.named_scope("ar3"):
         us = scale_rows(ar_total(3))
     for v in range(2):
         brow[v:v + 1] = live * us[v]
     brow[2:8] = jnp.zeros((6, NS), jnp.float32)
     arow[2:8] = jnp.zeros((6, NS), jnp.float32)
-    tile = pl.ds(pl.multiple_of((me // 4) * 128, 128), 128)
+    tile = pl.ds(pl.multiple_of((me // 4) * LANE, LANE), LANE)
     cols[0] = arow[:, tile].T
     cols[1] = brow[:, tile].T
     mine = pl.ds(pl.multiple_of(lax.rem(me, 4) * ROWS, ROWS), ROWS)
 
     def piece_row(owner, t, a):
-        return pl.multiple_of(owner * SH + t * CB + a * 128, 128)
+        return pl.multiple_of(owner * SH + t * CB + a * LANE, LANE)
 
     def parts_of(it):
         quad = (it + 8 - N2) // 8
@@ -273,7 +291,7 @@
         return t, par
 
     def push(owner, it, a, to, rsem):
-        ref = dc.at[pl.ds(piece_row(owner, parts_of(it)[0], a), 128)]
+        ref = dc.at[pl.ds(piece_row(owner, parts_of(it)[0], a), LANE)]
         send(ref, ref, ssem.at[it, a], rsem.at[it, a], to)
 
     def order(a):
@@ -284,22 +302,24 @@
         par = parts_of(it)[1]
         return holder + lax.rem(par, 2) * (d0 - me) + (par // 2) * (d1 - me)
 
-    def chunk(it):
+    def chunk(it, ready=False):
         t = parts_of(it)[0]
         owners = [owner_of(me, a, it) for a in range(3)]
-        c = jnp.concatenate([ca[pl.ds(piece_row(owners[a], t, a), 128)] for a in range(3)], axis=0)
+        c = jnp.concatenate([ca[pl.ds(piece_row(owners[a], t, a), LANE)] for a in range(3)], axis=0)
         wc = []
         for v in range(2):
             parts = []
             for a in range(3):
-                off = pl.multiple_of(t * CB + a * 128, 128)
-                row = wall[owners[a], pl.ds(v, 1), pl.ds(off, 128)] * gsc
-                parts.append(jnp.broadcast_to(row, (128, 128)).T)
+                off = pl.multiple_of(t * CB + a * LANE, LANE)
+                row = wall[owners[a], pl.ds(v, 1), pl.ds(off, LANE)] * gsc
+                parts.append(jnp.broadcast_to(row, (LANE, LANE)).T)
             wc.append(jnp.concatenate(parts, axis=0))
-        QR = 32
-        lanes = lax.broadcasted_iota(jnp.int32, (CB, 128), 1)
         HALF = CB // 2
-        LW = 256
+
+        def prob_at(s, v, q, l):
+            if ready:
+                return ex[v % 2, pl.ds(v // 2 * CB + QR * q, QR), pl.ds(LW * l, LW)]
+            return jnp.exp2(s[QR * q:QR * (q + 1), LW * l:LW * (l + 1)] * SCALE)
 
         def put_g(v, q, l, g):
             gt[v // 4, pl.ds(QR * q, QR), pl.ds((v % 4) * NS + LW * l, LW)] = g.astype(jnp.bfloat16)
@@ -311,40 +331,36 @@
         def rows_of(ref, v, l):
             return ref[v:v + 1, LW * l:LW * (l + 1)]
 
-        s0 = dot_nt(c, zall[0])
-        s1 = dot_nt(c, zall[1])
+        e0 = probs(c, 0) if not ready else None
+        e1 = probs(c, 1) if not ready else None
         for l in range(NS // LW):
             b0, b1, a0, a1 = rows_of(brow, 0, l), rows_of(brow, 1, l), rows_of(arow, 0, l), rows_of(arow, 1, l)
-            ln = slice(LW * l, LW * (l + 1))
             for q in range(CB // QR):
                 sl = slice(QR * q, QR * (q + 1))
-                p0 = jnp.exp2(s0[sl, ln] * SCALE)
-                p1 = jnp.exp2(s1[sl, ln] * SCALE)
+                p0 = prob_at(e0, 0, q, l)
+                p1 = prob_at(e1, 1, q, l)
                 x0 = (p0 * p0) * b0 * jnp.concatenate([wc[0][sl]] * 2, axis=1)
                 x1 = (p1 * p1) * b1 * jnp.concatenate([wc[1][sl]] * 2, axis=1)
                 xsc[pl.ds(QR * q, QR), pl.ds(LW * l, LW)] = x0 + x1
                 put_g(0, q, l, p0 * a0 - x1)
                 put_g(1, q, l, p1 * a1 - x0)
         res = None
-        for v in range(2, VIEWS):
-            sel = jnp.where(jnp.logical_and(lax.rem(lanes, 6) == v - 2, lanes < 18), 1.0, 0.0).astype(jnp.bfloat16)
-            s = dot_nt(jnp.concatenate([c, sel], axis=1), jnp.concatenate([zall[v], zt[...]], axis=1))
+        for v in SMALL:
+            e = probs(c, v) if not ready else None
             for l in range(NS // LW):
-                ln = slice(LW * l, LW * (l + 1))
                 for q in range(CB // QR):
-                    sl = slice(QR * q, QR * (q + 1))
-                    put_g(v, q, l, jnp.exp2(s[sl, ln] * SCALE) - xsc[pl.ds(QR * q, QR), pl.ds(LW * l, LW)])
+                    put_g(v, q, l, prob_at(e, v, q, l) - xsc[pl.ds(QR * q, QR), pl.ds(LW * l, LW)])
             if v == 3:
                 res = dc_part(0)
         more = dc_part(1)
         out = jnp.concatenate([res[0] + more[0], res[1] + more[1]], axis=0)
         for a in range(3):
-            dc[pl.ds(piece_row(owners[a], t, a), 128)] = out[128 * a:128 * (a + 1)]
+            dc[pl.ds(piece_row(owners[a], t, a), LANE)] = out[LANE * a:LANE * (a + 1)]
 
     def rows_part(i):
         ac = cols[0, mine]
         bc = cols[1, mine]
-        lanes = lax.broadcasted_iota(jnp.int32, (RB, 128), 1)
+        lanes = lax.broadcasted_iota(jnp.int32, (RB, LANE), 1)
         ones = jnp.where(lanes < 18, 1.0, 0.0).astype(jnp.bfloat16)
         for h in range(RPI):
             jb = i * RPI + h
@@ -353,9 +369,9 @@
             wr = []
             for v in range(2):
                 parts = []
-                for q in range(RB // 128):
-                    b = jb * (RB // 128) + q
-                    parts.append(wall[b // (SH // 128), pl.ds(v, 1), pl.ds(pl.multiple_of(lax.rem(b, SH // 128) * 128, 128), 128)])
+                for q in range(RB // LANE):
+                    b = jb * (RB // LANE) + q
+                    parts.append(wall[b // (SH // LANE), pl.ds(v, 1), pl.ds(pl.multiple_of(lax.rem(b, SH // LANE) * LANE, LANE), LANE)])
                 wr.append(jnp.concatenate(parts, axis=1))
             sv = [s[ROWS * v:ROWS * (v + 1)] for v in range(VIEWS)]
             p0 = jnp.exp2(sv[0])
@@ -373,12 +389,12 @@
             ssum = sv[2]
             for v in range(3, VIEWS):
                 ssum = ssum + sv[v]
-            for v in range(2, VIEWS):
+            for v in SMALL:
                 gr[pl.ds(v * ROWS, ROWS), col] = (jnp.exp2(sv[v]) - xs).astype(jnp.bfloat16)
             ls = x1 * sv[0] + x0 * sv[1] + xs * ssum
-            part = ls[:, 0:128]
-            for q in range(1, RB // 128):
-                part = part + ls[:, 128 * q:128 * (q + 1)]
+            part = ls[:, 0:LANE]
+            for q in range(1, RB // LANE):
+                part = part + ls[:, LANE * q:LANE * (q + 1)]
             acc[pl.ds(VIEWS * ROWS, ROWS)] += part
         cs = ca[pl.ds(pl.multiple_of(i * RW, RW), RW)]
         acc[pl.ds(0, VIEWS * ROWS)] += dot_nn(gr[...], cs)
@@ -396,7 +412,7 @@
     def serve2(it):
         for a in range(3):
             d0, d1, d2 = order(a)
-            drain(dc.at[pl.ds(0, 128)], r2.at[it, a])
+            drain(dc.at[pl.ds(0, LANE)], r2.at[it, a])
             o = owner_of(d1, a, it)
             push(o, it, a, d2, r3)
             push(o, it, a, sib, rs)
@@ -413,15 +429,15 @@
         @pl.when(it >= N2)
         def _():
             for a in range(3):
-                drain(dc.at[pl.ds(0, 128)], r3.at[it, a])
+                drain(dc.at[pl.ds(0, LANE)], r3.at[it, a])
                 push(owner_of(order(a)[2], a, it), it, a, sib, rs)
 
     with jax.named_scope("chunk0"):
-        chunk(0)
+        chunk(0, ready=True)
     own1(0)
     own(0)
     with jax.named_scope("wait_w"):
-        drain(wall.at[pl.ds(0, NDEV - 1)], wrecv)
+        drain(wall.at[pl.ds(0, OTHERS)], wrecv)
 
     def main(it, carry):
         with jax.named_scope("compute"):
@@ -457,7 +473,7 @@
     for v in range(2):
         qt[v] = qs[PARTS - 1, v, :, pl.ds(0, QT)]
     total = jnp.sum(jnp.sum(acc[pl.ds(VIEWS * ROWS, ROWS)], axis=1, keepdims=True), axis=0, keepdims=True)
-    slots[4, me] = jnp.broadcast_to(total, (8, 128))
+    slots[4, me] = jnp.broadcast_to(total, (8, LANE))
     ar_send(4)
 
     def last(it, carry):
@@ -476,26 +492,26 @@
         @pl.when(it < N2)
         def _():
             for a in range(3):
-                drain(dc.at[pl.ds(0, 4 * 128)], rs.at[it, a])
-                drain(dc.at[pl.ds(0, 7 * 128)], ssem.at[it, a])
+                drain(dc.at[pl.ds(0, 4 * LANE)], rs.at[it, a])
+                drain(dc.at[pl.ds(0, 7 * LANE)], ssem.at[it, a])
 
         @pl.when(it >= N2)
         def _():
             for a in range(3):
-                drain(dc.at[pl.ds(0, 2 * 128)], rs.at[it, a])
-                drain(dc.at[pl.ds(0, 3 * 128)], ssem.at[it, a])
+                drain(dc.at[pl.ds(0, 2 * LANE)], rs.at[it, a])
+                drain(dc.at[pl.ds(0, 3 * LANE)], ssem.at[it, a])
         return carry
 
     with jax.named_scope("finish"):
         lax.fori_loop(0, STEPS, finish, 0)
     drain(zall.at[pl.ds(0, 2), pl.ds(0, NS - ROWS)], zsend.at[0])
-    drain(zall.at[pl.ds(2, 6), pl.ds(0, 7 * ROWS)], zsend.at[1])
-    drain(zall.at[pl.ds(2, 6), pl.ds(0, 8 * ROWS)], zs2send)
-    drain(mrows.at[pl.ds(0, NDEV - 1)], arsend.at[0])
+    drain(zall.at[CROPS, pl.ds(0, 7 * ROWS)], zsend.at[1])
+    drain(zall.at[CROPS, pl.ds(0, 8 * ROWS)], zs2send)
+    drain(mrows.at[pl.ds(0, OTHERS)], arsend.at[0])
     for t in range(1, 5):
-        drain(slots.at[t, pl.ds(0, NDEV - 1)], arsend.at[t])
-    drain(lslots.at[pl.ds(0, NDEV - 1)], lsend)
-    drain(wall.at[pl.ds(0, NDEV - 1)], wsend)
+        drain(slots.at[t, pl.ds(0, OTHERS)], arsend.at[t])
+    drain(lslots.at[pl.ds(0, OTHERS)], lsend)
+    drain(wall.at[pl.ds(0, OTHERS)], wsend)
 
 
 def emit_kernel(dc, qs, qt, dz, loss, o_q1, o_q2, o_loss, o_z1, o_z2, o_zs, o_dc, sem):
@@ -508,7 +524,7 @@
                 pairs.append((qt.at[v], o.at[:, pl.ds(i * RW, QT)]))
         rows = pl.ds(i * RW, RW if i < PARTS - 1 else QT)
         pairs.append((dc.at[rows], o_dc.at[rows]))
-    pairs += [(loss, o_loss), (dz.at[0], o_z1), (dz.at[1], o_z2), (dz.at[pl.ds(2, 6)], o_zs)]
+    pairs += [(loss, o_loss), (dz.at[0], o_z1), (dz.at[1], o_z2), (dz.at[CROPS], o_zs)]
     copies = [pltpu.make_async_copy(a, b, sem.at[i]) for i, (a, b) in enumerate(pairs)]
     for c in copies:
         c.start()
@@ -529,11 +545,11 @@
                    vm((VIEWS, ROWS, D), f32), vm((1, 1), f32)],
         in_specs=[vmem] * 4 + [anym],
         out_specs=[vmem] * 5,
-        scratch_shapes=[vm((KPAD, D), bf16), vm((2, SH, NS), f32), vm((NDEV, 1, 128), f32), vm((5, NDEV, 8, 128), f32), vm((NDEV, 32, 128), f32),
+        scratch_shapes=[vm((KPAD, D), bf16), vm((2, SH, NS), f32), vm((NDEV, 1, LANE), f32), vm((5, NDEV, 8, LANE), f32), vm((NDEV, 32, LANE), f32),
                         vm((NDEV, 2, SH), f32), vm((VIEWS, NS, D), bf16), vm((8, NS), f32), vm((8, NS), f32),
                         vm((2, CB, 4 * NS), bf16), vm((CB, NS), f32),
-                        vm((VIEWS * ROWS, RW), bf16), vm((NS, 128), bf16), vm((3, 32, 128), f32), vm((VIEWS * ROWS, 2 * D), bf16),
-                        vm((2, 128, 8), f32),
+                        vm((VIEWS * ROWS, RW), bf16), vm((NS, LANE), bf16), vm((3, 32, LANE), f32), vm((VIEWS * ROWS, 2 * D), bf16),
+                        vm((2, LANE, 8), f32),
                         vm((VIEWS * ROWS + ROWS, D), f32),
                         dma, dma((2,)), dma, dma, dma, dma, dma((5,)), dma((5,)), dma, dma, dma, dma,
                         dma((STEPS, 3)), dma((STEPS, 3)), dma((STEPS, 3)), dma((STEPS, 3))],

time: 87.1 us -> 87.1 us (level)
  no operation moved by 1% of the time
where the time goes in v6:
time: 87.1 us; the launch traced here: 86.9 us
  Pallas kernels  86.1 us (99%)
    pallas_call x1, Pallas kernels, local_step(): pl.pallas_call(kernel, out_shape=[vm((KPAD, D), f32), vm((PARTS, 2, ROWS,...  77.3 us
    pallas_call x1, Pallas kernels, local_step(): pl.pallas_call(emit_kernel, out_shape=[jax.ShapeDtypeStruct((ROWS, KP), f...  8.78 us

profile of v6, /device:TPU:0, one launch (start us, length us, event | category | flops | bytes accessed | tf_op | source)
XLA Modules:
  0.0 86.9 jit_solution(18144669708449997965)
XLA Ops:
  0.6 77.3 %step.1 = (f32[30720,128]{1,0:T(8,128)S(1)}, f32[15,2,32,2048]{3,2,1,0:T(8,128)S(1)}, f32[2,32,1328]{2,1,0:T(8,128)S(1)}, f32[8,32,128]{2,1,0:T(8,128)S(1)}, f32[1,1]{1,0:T(1,128)}) custom-call(bf16[32,128]{1,0:T(8,128)(2,1)} %z1.1, bf16[32,128]{1,0:T(8,128)(2,1)} %z2.1, bf16[6,32,128]{2,1,0:T(8,128)(2,1)} %zs.1, s32[1,32]{1,0:T(1,128)} %bitcast.2, ...), custom_call_target="tpu_custom_call" | custom-call | tf_op jit(solution)/shard_map/step/pallas_call | solution.py:542
  78.0 8.8 %emit.1 = (f32[32,30000]{1,0:T(8,128)}, f32[32,30000]{1,0:T(8,128)}, f32[1,1]{1,0:T(1,128)}, f32[32,128]{1,0:T(8,128)}, f32[32,128]{1,0:T(8,128)}, /*index=5*/f32[6,32,128]{2,1,0:T(8,128)}, f32[30000,128]{1,0:T(8,128)}) custom-call(f32[30720,128]{1,0:T(8,128)S(1)} %get-tuple-element.19.dc, f32[15,2,32,2048]{3,2,1,0:T(8,128)S(1)} %get-tuple-element.20.qs, ...), custom_call_target="tpu_custom_call" | custom-call | tf_op jit(solution)/shard_map/emit/pallas_call | solution.py:559

commit v7 on v6

--- a/solution.py
+++ b/solution.py
@@ -57,13 +57,6 @@
     return me + bit - 2 * bit * lax.rem(me // bit, 2)
 
 
-def full_barrier(me):
-    barrier = pltpu.get_barrier_semaphore()
-    for d in PEERS:
-        pl.semaphore_signal(barrier, inc=1, device_id=lax.rem(me + d, NDEV), device_id_type=LOGICAL)
-    pl.semaphore_wait(barrier, OTHERS)
-
-
 def send(src, dst, ssem, rsem, to):
     copy = pltpu.make_async_remote_copy(src_ref=src, dst_ref=dst, send_sem=ssem, recv_sem=rsem,
                                         device_id=to, device_id_type=LOGICAL)
@@ -75,20 +68,29 @@
 
 
 def kernel(z1, z2, zs, mask, protos, dc, qs, qt, dz, loss,
-           ca, ex, mrows, slots, lslots, wall, zall, arow, brow, gt, xsc, gr, zt, px, zl, cols, acc,
-           csem, zsend, zlrecv, zs1recv, zs2send, zs2recv, arsend, arrecv, lsend, lrecv, wsend, wrecv,
+           ca, ex, mrows, slots, lslots, wall, zall, arow, brow, gt, xsc, gr, zt, px, zl, cols, acc, mv,
+           insem, msem, csem, zsend, zlrecv, zs1recv, zs2send, zs2recv, arsend, arrecv, lsend, lrecv, wsend, wrecv,
            ssem, r2, r3, rs):
     me = lax.axis_index("data")
+    barrier = pltpu.get_barrier_semaphore()
+    for d in PEERS:
+        pl.semaphore_signal(barrier, inc=1, device_id=lax.rem(me + d, NDEV), device_id_type=LOGICAL)
+    myrows = pl.ds(pl.multiple_of(me * ROWS, ROWS), ROWS)
+    ins = [pltpu.make_async_copy(src, dst, insem.at[i]) for i, (src, dst) in enumerate((
+        (mask, mv), (z1, zall.at[0, myrows]), (z2, zall.at[1, myrows]), (zs, zall.at[CROPS, myrows])))]
+    for c in ins:
+        c.start()
     cc = pltpu.make_async_copy(protos, ca.at[pl.ds(0, KP)], csem)
     cc.start()
-    ca[pl.ds(KP, KPAD - KP), :] = jnp.zeros((KPAD - KP, D), jnp.bfloat16)
     dims = (flip(me, 2), flip(me, 4), flip(me, 8))
     sib = flip(me, 1)
-    mpad = jnp.concatenate([mask[...].astype(jnp.float32), jnp.zeros((1, LANE - ROWS), jnp.float32)], axis=1)
+    ins[0].wait()
+    mpad = jnp.concatenate([mv[...].astype(jnp.float32), jnp.zeros((1, LANE - ROWS), jnp.float32)], axis=1)
     mrows[me] = pltpu.roll(jnp.broadcast_to(mpad, (8, LANE)), ROWS * lax.rem(me, 4), 1)[0:1]
+    for c in ins[1:]:
+        c.wait()
     with jax.named_scope("barrier"):
-        full_barrier(me)
-    myrows = pl.ds(pl.multiple_of(me * ROWS, ROWS), ROWS)
+        pl.semaphore_wait(barrier, OTHERS)
 
     def ar_send(t):
         for d in PEERS:
@@ -102,31 +104,31 @@
         return tot
 
     for d in PEERS:
-        to = lax.rem(me + d, NDEV)
-        send(z1, zall.at[0, myrows], zsend.at[0], zlrecv, to)
-        send(z2, zall.at[1, myrows], zsend.at[0], zlrecv, to)
+        send(zall.at[0, myrows], zall.at[0, myrows], zsend.at[0], zlrecv.at[0], lax.rem(me + d, NDEV))
     for d in PEERS:
-        send(mrows.at[me], mrows.at[me], arsend.at[0], arrecv.at[0], lax.rem(me + d, NDEV))
+        send(mrows.at[me], mrows.at[me], msem.at[0], msem.at[1], lax.rem(me + d, NDEV))
+    for d in PEERS:
+        send(zall.at[1, myrows], zall.at[1, myrows], zsend.at[1], zlrecv.at[1], lax.rem(me + d, NDEV))
     for d in PEERS_HALF:
-        send(zs, zall.at[CROPS, myrows], zsend.at[1], zs1recv, lax.rem(me + 2 * d, NDEV))
-    zall[0, myrows] = z1[...]
-    zall[1, myrows] = z2[...]
-    zall[CROPS, myrows] = zs[...]
-    send(zs, zall.at[CROPS, myrows], zs2send, zs2recv, sib)
-    zl[pl.ds(0, ROWS), pl.ds(0, D)] = z1[...]
-    zl[pl.ds(ROWS, ROWS), pl.ds(0, D)] = z2[...]
-    zl[pl.ds(2 * ROWS, 6 * ROWS), pl.ds(0, D)] = zs[...].reshape(6 * ROWS, D)
+        send(zall.at[CROPS, myrows], zall.at[CROPS, myrows], zsend.at[2], zs1recv, lax.rem(me + 2 * d, NDEV))
+    send(zall.at[CROPS, myrows], zall.at[CROPS, myrows], zs2send, zs2recv, sib)
+    zl[pl.ds(0, ROWS), pl.ds(0, D)] = zall[0, myrows]
+    zl[pl.ds(ROWS, ROWS), pl.ds(0, D)] = zall[1, myrows]
+    zl[pl.ds(2 * ROWS, 6 * ROWS), pl.ds(0, D)] = zall[CROPS, myrows].reshape(6 * ROWS, D)
     zl[pl.ds(0, 2 * ROWS), pl.ds(D, LANE)] = jnp.zeros((2 * ROWS, LANE), jnp.bfloat16)
+    ca[pl.ds(KP, KPAD - KP), :] = jnp.zeros((KPAD - KP, D), jnp.bfloat16)
     acc[...] = jnp.zeros_like(acc)
     cc.wait()
     with jax.named_scope("mask"):
-        drain(mrows.at[pl.ds(0, OTHERS)], arrecv.at[0])
+        drain(mrows.at[pl.ds(0, OTHERS)], msem.at[1])
         mask8 = [mrows[4 * j] + mrows[4 * j + 1] + mrows[4 * j + 2] + mrows[4 * j + 3] for j in range(4)]
     mask4 = jnp.concatenate(mask8, axis=0)
     mrow = jnp.concatenate(mask8, axis=1)
     live = jnp.sum(jnp.sum(mask4, axis=1, keepdims=True), axis=0, keepdims=True)
-    with jax.named_scope("zlarge"):
-        drain(zall.at[pl.ds(0, 2), pl.ds(0, NS - ROWS)], zlrecv)
+
+    def zwait(v):
+        with jax.named_scope("zlarge"):
+            drain(zall.at[0, pl.ds(0, NS - ROWS)], zlrecv.at[v])
 
     def shard(b):
         return ca[pl.ds(pl.multiple_of(me * SH + b * CB, LANE), CB)]
@@ -137,32 +139,25 @@
 
     zero8 = jnp.zeros((8, NS), jnp.float32)
 
-    def first(b, carry):
-        rows = pl.ds(b * CB, CB)
-        out = []
-        for v in range(2):
-            ps, r = carry[2 * v], carry[2 * v + 1]
+    def first(v):
+        ps, r = zero8, zero8
+        for b in range(NCH):
             p = jnp.exp2(dot_nt(shard(b), zall[v]) * SCALE)
             ps = ps + fold8(p)
             e = p * p * mrow
-            ex[v, rows] = e
+            ex[v, pl.ds(b * CB, CB)] = e
             w = col_scale(jnp.sum(e, axis=1, keepdims=True), b)
             r = r + fold8(e * w)
-            out += [ps, r]
-        return tuple(out)
-
-    def put(t, r1, r2):
-        for v, r in enumerate((r1, r2)):
-            row = jnp.sum(r, axis=0, keepdims=True)
-            for j in range(4):
-                slots[t, me, pl.ds(4 * v + j, 1)] = row[:, LANE * j:LANE * (j + 1)]
-
-    def scale_rows(tot):
-        us = []
-        for v in range(2):
-            r = jnp.concatenate([tot[4 * v + j:4 * v + j + 1] for j in range(4)], axis=1)
-            us.append(mrow / (live * jnp.where(mrow > 0, r, 1.0)))
-        return us
+        return ps, r
+
+    def put(t, r):
+        row = jnp.sum(r, axis=0, keepdims=True)
+        for j in range(4):
+            slots[t, me, pl.ds(j, 1)] = row[:, LANE * j:LANE * (j + 1)]
+
+    def scale_row(tot):
+        r = jnp.concatenate([tot[j:j + 1] for j in range(4)], axis=1)
+        return mrow / (live * jnp.where(mrow > 0, r, 1.0))
 
     pad = jnp.where(me == OTHERS, float(SH - LAST), 0.0)
 
@@ -171,15 +166,19 @@
         for j in range(4):
             lslots[me, pl.ds(4 * v + j, 1)] = row[:, LANE * j:LANE * (j + 1)]
 
-    with jax.named_scope("first"):
-        carry = (zero8,) * 4
-        for b in range(NCH):
-            carry = first(b, carry)
-        ps1, r1, ps2, rr2 = carry
-        put(1, r1, rr2)
-        ar_send(1)
-    put_lse(0, ps1)
-    put_lse(1, ps2)
+    def lse_send(k):
+        ref = lslots.at[me, pl.ds(8 * k, 8)]
+        for d in PEERS:
+            send(ref, ref, lsend.at[k], lrecv.at[k], lax.rem(me + d, NDEV))
+
+    for v in range(2):
+        zwait(v)
+        with jax.named_scope("first"):
+            ps, r = first(v)
+            put(v, r)
+            ar_send(v)
+        put_lse(v, ps)
+    lse_send(0)
     with jax.named_scope("zsmall1"):
         drain(zall.at[CROPS, pl.ds(0, 7 * ROWS)], zs1recv)
     for d in PEERS_HALF:
@@ -194,48 +193,41 @@
         put_lse(v, ps)
         return carry
 
+    def again(v, t):
+        with jax.named_scope("ar%d" % t):
+            u = scale_row(ar_total(t - 2))
+        last = t > 3
+
+        def step(b, r):
+            rows = pl.ds(pl.multiple_of(b * CB, CB), CB)
+            e = ex[v, rows]
+            w = col_scale(jnp.sum(e * u, axis=1, keepdims=True), b)
+            if last:
+                for q in range(CB // LANE):
+                    wt = jnp.broadcast_to(w[LANE * q:LANE * (q + 1)], (LANE, LANE)).T
+                    wall[me, pl.ds(v, 1), pl.ds(pl.multiple_of(b * CB + LANE * q, LANE), LANE)] = wt[0:1]
+            return r + fold8(e * w)
+
+        with jax.named_scope("again%d" % t):
+            put(t, lax.fori_loop(0, NCH, step, zero8))
+            ar_send(t)
+
+    again(0, 2)
+    again(1, 3)
     with jax.named_scope("zsmall2"):
         drain(zall.at[CROPS, pl.ds(0, 8 * ROWS)], zs2recv)
-
     with jax.named_scope("small"):
-        lax.fori_loop(0, 3, small, 0)
-    with jax.named_scope("ar1"):
-        us = scale_rows(ar_total(1))
-
-    def again(us, last):
-        def step(b, carry):
-            rows = pl.ds(pl.multiple_of(b * CB, CB), CB)
-            out = []
-            for v in range(2):
-                e = ex[v, rows]
-                w = col_scale(jnp.sum(e * us[v], axis=1, keepdims=True), b)
-                out.append(carry[v] + fold8(e * w))
-                if last:
-                    for q in range(CB // LANE):
-                        wt = jnp.broadcast_to(w[LANE * q:LANE * (q + 1)], (LANE, LANE)).T
-                        wall[me, pl.ds(v, 1), pl.ds(pl.multiple_of(b * CB + LANE * q, LANE), LANE)] = wt[0:1]
-            return tuple(out)
-        return step
-
-    with jax.named_scope("again2"):
-        r1, rr2 = lax.fori_loop(0, NCH, again(us, False), (zero8, zero8))
-        put(2, r1, rr2)
-        ar_send(2)
-    with jax.named_scope("small"):
-        lax.fori_loop(3, 6, small, 0)
-        for d in PEERS:
-            send(lslots.at[me], lslots.at[me], lsend, lrecv, lax.rem(me + d, NDEV))
-    with jax.named_scope("ar2"):
-        us = scale_rows(ar_total(2))
-    with jax.named_scope("again3"):
-        r1, rr2 = lax.fori_loop(0, NCH, again(us, True), (zero8, zero8))
-        put(3, r1, rr2)
-        ar_send(3)
-        for d in PEERS:
-            send(wall.at[me], wall.at[me], wsend, wrecv, lax.rem(me + d, NDEV))
+        for k in range(1, 4):
+            lax.fori_loop(2 * k - 2, 2 * k, small, 0)
+            lse_send(k)
+    again(0, 4)
+    again(1, 5)
+    for d in PEERS:
+        send(wall.at[me], wall.at[me], wsend, wrecv, lax.rem(me + d, NDEV))
     gsc = 1.0 / (TAU * PAIRS * live)
     with jax.named_scope("lse"):
-        drain(lslots.at[pl.ds(0, OTHERS)], lrecv)
+        for k in range(4):
+            drain(lslots.at[pl.ds(0, OTHERS), pl.ds(0, 8)], lrecv.at[k])
         tot = lslots[0]
         for i in PEERS:
             tot = tot + lslots[i]
@@ -271,7 +263,7 @@
         for v in range(VIEWS):
             ex[v % 2, pl.ds(v // 2 * CB, CB)] = jnp.exp2(probs(shard(0), v) * SCALE)
     with jax.named_scope("ar3"):
-        us = scale_rows(ar_total(3))
+        us = [scale_row(ar_total(4)), scale_row(ar_total(5))]
     for v in range(2):
         brow[v:v + 1] = live * us[v]
     brow[2:8] = jnp.zeros((6, NS), jnp.float32)
@@ -473,8 +465,8 @@
     for v in range(2):
         qt[v] = qs[PARTS - 1, v, :, pl.ds(0, QT)]
     total = jnp.sum(jnp.sum(acc[pl.ds(VIEWS * ROWS, ROWS)], axis=1, keepdims=True), axis=0, keepdims=True)
-    slots[4, me] = jnp.broadcast_to(total, (8, LANE))
-    ar_send(4)
+    slots[6, me] = jnp.broadcast_to(total, (4, LANE))
+    ar_send(6)
 
     def last(it, carry):
         with jax.named_scope("serve3"):
@@ -484,7 +476,7 @@
     lax.fori_loop(STEPS - LAG3, STEPS, last, 0)
     dz[...] = acc[pl.ds(0, VIEWS * ROWS)].reshape(VIEWS, ROWS, D)
     with jax.named_scope("loss"):
-        tot = ar_total(4)
+        tot = ar_total(6)
     cross = tot[0:1, 0:1] * (LN2 * TAU * PAIRS) * live - lsum
     loss[...] = -cross / (live * PAIRS)
 
@@ -504,13 +496,15 @@
 
     with jax.named_scope("finish"):
         lax.fori_loop(0, STEPS, finish, 0)
-    drain(zall.at[pl.ds(0, 2), pl.ds(0, NS - ROWS)], zsend.at[0])
-    drain(zall.at[CROPS, pl.ds(0, 7 * ROWS)], zsend.at[1])
+    for v in range(2):
+        drain(zall.at[0, pl.ds(0, NS - ROWS)], zsend.at[v])
+    drain(zall.at[CROPS, pl.ds(0, 7 * ROWS)], zsend.at[2])
     drain(zall.at[CROPS, pl.ds(0, 8 * ROWS)], zs2send)
-    drain(mrows.at[pl.ds(0, OTHERS)], arsend.at[0])
-    for t in range(1, 5):
+    drain(mrows.at[pl.ds(0, OTHERS)], msem.at[0])
+    for t in range(7):
         drain(slots.at[t, pl.ds(0, OTHERS)], arsend.at[t])
-    drain(lslots.at[pl.ds(0, OTHERS)], lsend)
+    for k in range(4):
+        drain(lslots.at[pl.ds(0, OTHERS), pl.ds(0, 8)], lsend.at[k])
     drain(wall.at[pl.ds(0, OTHERS)], wsend)
 
 
@@ -543,15 +537,16 @@
         kernel,
         out_shape=[vm((KPAD, D), f32), vm((PARTS, 2, ROWS, RW), f32), vm((2, ROWS, QT), f32),
                    vm((VIEWS, ROWS, D), f32), vm((1, 1), f32)],
-        in_specs=[vmem] * 4 + [anym],
+        in_specs=[anym] * 5,
         out_specs=[vmem] * 5,
-        scratch_shapes=[vm((KPAD, D), bf16), vm((2, SH, NS), f32), vm((NDEV, 1, LANE), f32), vm((5, NDEV, 8, LANE), f32), vm((NDEV, 32, LANE), f32),
+        scratch_shapes=[vm((KPAD, D), bf16), vm((2, SH, NS), f32), vm((NDEV, 1, LANE), f32), vm((7, NDEV, 4, LANE), f32), vm((NDEV, 32, LANE), f32),
                         vm((NDEV, 2, SH), f32), vm((VIEWS, NS, D), bf16), vm((8, NS), f32), vm((8, NS), f32),
                         vm((2, CB, 4 * NS), bf16), vm((CB, NS), f32),
                         vm((VIEWS * ROWS, RW), bf16), vm((NS, LANE), bf16), vm((3, 32, LANE), f32), vm((VIEWS * ROWS, 2 * D), bf16),
                         vm((2, LANE, 8), f32),
                         vm((VIEWS * ROWS + ROWS, D), f32),
-                        dma, dma((2,)), dma, dma, dma, dma, dma((5,)), dma((5,)), dma, dma, dma, dma,
+                        vm((1, ROWS), jnp.int32),
+                        dma((4,)), dma((2,)), dma, dma((3,)), dma((2,)), dma, dma, dma, dma((7,)), dma((7,)), dma((4,)), dma((4,)), dma, dma,
                         dma((STEPS, 3)), dma((STEPS, 3)), dma((STEPS, 3)), dma((STEPS, 3))],
         compiler_params=pltpu.CompilerParams(collective_id=0, has_side_effects=True, vmem_limit_bytes=VM),
         name="step",

time: 87.1 us -> 85.5 us (0.982)
  Pallas kernels: 86.1 us -> 84.5 us
    pallas_call x1, Pallas kernels: 77.3 us -> 75.7 us  [local_step(): pl.pallas_call(kernel, out_shape=[vm((KPAD, D), f32), vm((PARTS, 2, ROWS,...]
where the time goes in v7:
time: 85.5 us; the launch traced here: 85.3 us
  Pallas kernels  84.5 us (99%)
    pallas_call x1, Pallas kernels, local_step(): pl.pallas_call(kernel, out_shape=[vm((KPAD, D), f32), vm((PARTS, 2, ROWS,...  75.7 us
    pallas_call x1, Pallas kernels, local_step(): pl.pallas_call(emit_kernel, out_shape=[jax.ShapeDtypeStruct((ROWS, KP), f...  8.78 us

profile of v7, /device:TPU:0, one launch (start us, length us, event | category | flops | bytes accessed | tf_op | source)
XLA Modules:
  0.0 85.3 jit_solution(4319649892996984663)
XLA Ops:
  0.6 75.7 %step.1 = (f32[30720,128]{1,0:T(8,128)S(1)}, f32[15,2,32,2048]{3,2,1,0:T(8,128)S(1)}, f32[2,32,1328]{2,1,0:T(8,128)S(1)}, f32[8,32,128]{2,1,0:T(8,128)S(1)}, f32[1,1]{1,0:T(1,128)}) custom-call(bf16[32,128]{1,0:T(8,128)(2,1)} %z1.1, bf16[32,128]{1,0:T(8,128)(2,1)} %z2.1, bf16[6,32,128]{2,1,0:T(8,128)(2,1)} %zs.1, s32[1,32]{1,0:T(1,128)} %bitcast.2, ...), custom_call_target="tpu_custom_call" | custom-call | tf_op jit(solution)/shard_map/step/pallas_call | solution.py:536
  76.4 8.8 %emit.1 = (f32[32,30000]{1,0:T(8,128)}, f32[32,30000]{1,0:T(8,128)}, f32[1,1]{1,0:T(1,128)}, f32[32,128]{1,0:T(8,128)}, f32[32,128]{1,0:T(8,128)}, /*index=5*/f32[6,32,128]{2,1,0:T(8,128)}, f32[30000,128]{1,0:T(8,128)}) custom-call(f32[30720,128]{1,0:T(8,128)S(1)} %get-tuple-element.19.dc, f32[15,2,32,2048]{3,2,1,0:T(8,128)S(1)} %get-tuple-element.20.qs, ...), custom_call_target="tpu_custom_call" | custom-call | tf_op jit(solution)/shard_map/emit/pallas_call | solution.py:554

commit v8 on v7

--- a/solution.py
+++ b/solution.py
@@ -28,6 +28,7 @@
 N2 = 2 * (NCH - NQ)
 STEPS = N2 + 4 * NQ
 PARTS = 15
+ALONE = 3
 RPI = KPAD // RB // PARTS
 RW = RPI * RB
 QT = KP - RW * (PARTS - 1)
@@ -431,10 +432,11 @@
     with jax.named_scope("wait_w"):
         drain(wall.at[pl.ds(0, OTHERS)], wrecv)
 
-    def main(it, carry):
+    def main(it, with_rows):
         with jax.named_scope("compute"):
             chunk(it)
-            rows_part(it - 1)
+            if with_rows:
+                rows_part(it - ALONE)
 
         @pl.when(it < N2)
         def _():
@@ -452,16 +454,23 @@
             with jax.named_scope("serve3"):
                 serve3(it - LAG3)
 
+    def main_alone(it, carry):
+        main(it, False)
         return carry
 
-    lax.fori_loop(1, STEPS, main, 0)
+    def main_rows(it, carry):
+        main(it, True)
+        return carry
+
+    lax.fori_loop(1, ALONE, main_alone, 0)
+    lax.fori_loop(ALONE, STEPS, main_rows, 0)
 
     def rest(i, carry):
         with jax.named_scope("rows"):
             rows_part(i)
         return carry
 
-    lax.fori_loop(STEPS - 1, PARTS, rest, 0)
+    lax.fori_loop(STEPS - ALONE, PARTS, rest, 0)
     for v in range(2):
         qt[v] = qs[PARTS - 1, v, :, pl.ds(0, QT)]
     total = jnp.sum(jnp.sum(acc[pl.ds(VIEWS * ROWS, ROWS)], axis=1, keepdims=True), axis=0, keepdims=True)

time: 85.5 us -> 84.7 us (level)
  no operation moved by 1% of the time
where the time goes in v8:
time: 84.7 us; the launch traced here: 84.6 us
  Pallas kernels  83.8 us (99%)
    pallas_call x1, Pallas kernels, local_step(): pl.pallas_call(kernel, out_shape=[vm((KPAD, D), f32), vm((PARTS, 2, ROWS,...  75 us
    pallas_call x1, Pallas kernels, local_step(): pl.pallas_call(emit_kernel, out_shape=[jax.ShapeDtypeStruct((ROWS, KP), f...  8.78 us

profile of v8, /device:TPU:0, one launch (start us, length us, event | category | flops | bytes accessed | tf_op | source)
XLA Modules:
  0.0 84.6 jit_solution(2935872656495655189)
XLA Ops:
  0.6 75.0 %step.1 = (f32[30720,128]{1,0:T(8,128)S(1)}, f32[15,2,32,2048]{3,2,1,0:T(8,128)S(1)}, f32[2,32,1328]{2,1,0:T(8,128)S(1)}, f32[8,32,128]{2,1,0:T(8,128)S(1)}, f32[1,1]{1,0:T(1,128)}) custom-call(bf16[32,128]{1,0:T(8,128)(2,1)} %z1.1, bf16[32,128]{1,0:T(8,128)(2,1)} %z2.1, bf16[6,32,128]{2,1,0:T(8,128)(2,1)} %zs.1, s32[1,32]{1,0:T(1,128)} %bitcast.2, ...), custom_call_target="tpu_custom_call" | custom-call | tf_op jit(solution)/shard_map/step/pallas_call | solution.py:545
  75.6 8.8 %emit.1 = (f32[32,30000]{1,0:T(8,128)}, f32[32,30000]{1,0:T(8,128)}, f32[1,1]{1,0:T(1,128)}, f32[32,128]{1,0:T(8,128)}, f32[32,128]{1,0:T(8,128)}, /*index=5*/f32[6,32,128]{2,1,0:T(8,128)}, f32[30000,128]{1,0:T(8,128)}) custom-call(f32[30720,128]{1,0:T(8,128)S(1)} %get-tuple-element.19.dc, f32[15,2,32,2048]{3,2,1,0:T(8,128)S(1)} %get-tuple-element.20.qs, ...), custom_call_target="tpu_custom_call" | custom-call | tf_op jit(solution)/shard_map/emit/pallas_call | solution.py:563

commit v9 on v8

--- a/solution.py
+++ b/solution.py
@@ -471,11 +471,11 @@
         return carry
 
     lax.fori_loop(STEPS - ALONE, PARTS, rest, 0)
-    for v in range(2):
-        qt[v] = qs[PARTS - 1, v, :, pl.ds(0, QT)]
     total = jnp.sum(jnp.sum(acc[pl.ds(VIEWS * ROWS, ROWS)], axis=1, keepdims=True), axis=0, keepdims=True)
     slots[6, me] = jnp.broadcast_to(total, (4, LANE))
     ar_send(6)
+    for v in range(2):
+        qt[v] = qs[PARTS - 1, v, :, pl.ds(0, QT)]
 
     def last(it, carry):
         with jax.named_scope("serve3"):

time: 84.7 us -> 84.7 us (level)
  no operation moved by 1% of the time
where the time goes in v9:
time: 84.7 us; the launch traced here: 84.6 us
  Pallas kernels  83.8 us (99%)
    pallas_call x1, Pallas kernels, local_step(): pl.pallas_call(kernel, out_shape=[vm((KPAD, D), f32), vm((PARTS, 2, ROWS,...  75 us
    pallas_call x1, Pallas kernels, local_step(): pl.pallas_call(emit_kernel, out_shape=[jax.ShapeDtypeStruct((ROWS, KP), f...  8.78 us

profile of v9, /device:TPU:0, one launch (start us, length us, event | category | flops | bytes accessed | tf_op | source)
XLA Modules:
  0.0 84.6 jit_solution(8497516702785864072)
XLA Ops:
  0.6 75.0 %step.1 = (f32[30720,128]{1,0:T(8,128)S(1)}, f32[15,2,32,2048]{3,2,1,0:T(8,128)S(1)}, f32[2,32,1328]{2,1,0:T(8,128)S(1)}, f32[8,32,128]{2,1,0:T(8,128)S(1)}, f32[1,1]{1,0:T(1,128)}) custom-call(bf16[32,128]{1,0:T(8,128)(2,1)} %z1.1, bf16[32,128]{1,0:T(8,128)(2,1)} %z2.1, bf16[6,32,128]{2,1,0:T(8,128)(2,1)} %zs.1, s32[1,32]{1,0:T(1,128)} %bitcast.2, ...), custom_call_target="tpu_custom_call" | custom-call | tf_op jit(solution)/shard_map/step/pallas_call | solution.py:545
  75.6 8.8 %emit.1 = (f32[32,30000]{1,0:T(8,128)}, f32[32,30000]{1,0:T(8,128)}, f32[1,1]{1,0:T(1,128)}, f32[32,128]{1,0:T(8,128)}, f32[32,128]{1,0:T(8,128)}, /*index=5*/f32[6,32,128]{2,1,0:T(8,128)}, f32[30000,128]{1,0:T(8,128)}) custom-call(f32[30720,128]{1,0:T(8,128)S(1)} %get-tuple-element.19.dc, f32[15,2,32,2048]{3,2,1,0:T(8,128)S(1)} %get-tuple-element.20.qs, ...), custom_call_target="tpu_custom_call" | custom-call | tf_op jit(solution)/shard_map/emit/pallas_call | solution.py:563
